TPU v7x, 256 devices: a whole 4x4x8 slice. The times are simulated.
256 devices in a mesh: ang: 32 (over y, z_hi, x), slab: 8 (over z_lo, core).
Axes of the slice: x: 4, y: 4, z: 8 (z_hi: 2, z_lo: 4; z = z_hi * 4 + z_lo), core: 2. Of those that a mesh axis runs over, the one named last changes fastest.
Arguments:
- updates: float32 [128, 2, 1024, 512], P('ang', None, 'slab'), may hold values from -6 to 6
- interp_tiles: bfloat16 [128, 32, 256, 128], P('ang'), may hold values from -0.25 to 0.25
- band_start: int32 [128, 32], P('ang'), may hold values from 0 to 2
- angle_id: int32 [128], P('ang'), may hold values from 0 to 127, each once
- angle_weight: float32 [128], replicated, may hold values from 0.05 to 0.5
- volume: float32 [4096, 2, 1024], P('ang', None, 'slab'), may hold values from -6 to 6
Outputs:
- volume_next: float32 [4096, 2, 1024], P('ang', None, 'slab')
- projection: float32 [128, 2, 1024, 512], P('ang', None, 'slab')
Inputs may be any that keep to these rules, and one draw needn't show every extreme that they name: Tile j of angle slot a reads detector columns 128 * band_start[a, j] up to 256 further. `angle_id`: each measured angle stands in exactly one slot.
All inputs are finite; a program needn't handle non-finite values.
Results may differ from a plain program's by a relative error of at most 0.0062.
Values may be sent and summed in bfloat16 or wider, within the bound.
No kernel may reach another device: no remote copies, remote signals or barrier semaphores. Data moves between devices by JAX's collectives and lax.ppermute only.
A program may use at most 128 MiB of HBM per device.

v0:
```python
import functools

import jax
import jax.numpy as jnp
from jax import lax
from jax.experimental import pallas as pl
from jax.experimental.pallas import tpu as pltpu
from jax.sharding import PartitionSpec as P


SMOOTHING = 0.25
YS, ZS, XS = 4, 2, 4
LINE = 4
FAR = (2, 1, 3)
ORDER = [(other, d) for d in (*FAR, 0) for other in (1, 0)]


def moves(other, first, delta):
    pairs = []
    for y in range(YS):
        for zh in range(ZS):
            for x in range(XS):
                along_x = (zh ^ other == 0) == first
                ty, tx = (y, (x + delta) % XS) if along_x else ((y + delta) % YS, x)
                pairs.append(((y * ZS + zh) * XS + x, (ty * ZS + zh) * XS + tx))
    return pairs


def moved(value, other, first, delta):
    return lax.ppermute(value, "ang", moves(other, first, delta))


def place(other, d):
    return ORDER.index((other, d)) * LINE


def across(value):
    half = [(a, a ^ XS) for a in range(YS * ZS * XS)]
    return lax.ppermute(value, "ang", half)


def params(mib, **more):
    return pltpu.CompilerParams(vmem_limit_bytes=mib << 20, **more)


VMEM = pl.BlockSpec(memory_space=pltpu.VMEM)
SMEM = pl.BlockSpec(memory_space=pltpu.SMEM)


AHEAD = pl.CostEstimate(flops=1 << 33, bytes_accessed=1 << 20, transcendentals=0)


def call(kernel, in_specs, outs, flops, mib=16):
    return pl.pallas_call(
        kernel,
        in_specs=in_specs,
        out_specs=[VMEM] * len(outs),
        out_shape=[jax.ShapeDtypeStruct(shape, dtype) for shape, dtype in outs],
        compiler_params=params(mib),
        cost_estimate=pl.CostEstimate(flops=flops, bytes_accessed=1 << 20, transcendentals=0),
    )


def plan_kernel(table):
    me = lax.axis_index("ang")
    y, zh, x = lax.shift_right_logical(me, 3), lax.shift_right_logical(me, 2) & 1, me & 3
    for i, (other, d, k) in enumerate((o, d, k) for o, d in ORDER for k in range(LINE)):
        owner = zh ^ other
        dy = k + owner * (d - k)
        dx = d + owner * (k - d)
        table[i] = ((y + dy) & 3) * 8 + owner * 4 + ((x + dx) & 3)


def plan():
    return pl.pallas_call(
        plan_kernel,
        out_specs=SMEM,
        out_shape=jax.ShapeDtypeStruct((len(ORDER) * LINE,), jnp.int32),
        compiler_params=params(4),
        cost_estimate=AHEAD,
        name="plan",
    )()


def edges_kernel(table, volume, cells, head, tail):
    depth = volume.shape[2]
    for c in range(2):
        turned = volume[:, c, :].T
        cells[c * depth : (c + 1) * depth, :] = turned
        head[c : c + 1, :] = turned[:1, :]
        tail[c : c + 1, :] = turned[depth - 1 :, :]


def edges(volume, table):
    share, _, depth = volume.shape
    outs = [((2 * depth, share), jnp.float32)] + [((2, share), jnp.float32)] * 2
    return call(edges_kernel, [SMEM, VMEM], outs, 1 << 20, 4)(table, volume)


def product(scaled, held, starts, j):
    angles, _, _ = scaled.shape
    block = held.shape[3]
    windows = []
    for a in range(angles):
        start = pl.multiple_of(starts[a, j] * block, block)
        windows.append(scaled[a, :, pl.ds(start, 2 * block)])
    return jnp.dot(
        jnp.concatenate(windows, axis=1),
        jnp.concatenate([held[a, j] for a in range(angles)], axis=0),
        preferred_element_type=jnp.float32,
    )


def scale_kernel(table, ids, weights, updates, scaled):
    depth = updates.shape[2]
    for a in range(updates.shape[0]):
        weight = weights[ids[a]]
        for c in range(2):
            at = slice(c * depth, (c + 1) * depth)
            scaled[a, at, :] = (weight * updates[a, c]).astype(jnp.bfloat16)


def scale(updates, table, ids, weights):
    angles, _, depth, detector = updates.shape
    outs = [((angles, 2 * depth, detector), jnp.bfloat16)]
    return call(scale_kernel, [SMEM, SMEM, SMEM, VMEM], outs, 1 << 33, 8)(
        table, ids, weights, updates
    )[0]


def back_kernel(base, table, starts, scaled, held, after, *outs):
    for g, out in enumerate(outs):
        for k in range(LINE):
            i = base + g * LINE + k
            out[k] = product(scaled, held, starts, table[i]).astype(out.dtype)


def back(scaled, held, table, starts, d, dtype, after):
    _, rows, _ = scaled.shape
    angles, _, band, block = held.shape
    outs = [((LINE, rows, block), dtype)] * 2
    flops = 2 * len(outs) * LINE * angles * rows * band * block
    kernel = functools.partial(back_kernel, place(1, d))
    specs = [SMEM, SMEM, VMEM, VMEM, pl.BlockSpec(memory_space=pl.ANY)]
    return call(kernel, specs, outs, flops)(table, starts, scaled, held, after)


def line_kernel(own, s1, s2, s3, kept, *sent):
    for k in range(LINE):
        total = own[k]
        for ref in (s1, s2, s3):
            total = total + ref[k].astype(jnp.float32)
        if k == 0:
            kept[...] = total
        else:
            sent[k - 1][...] = total.astype(jnp.bfloat16)


def line_sum(own, arrived):
    tile = own.shape[1:]
    outs = [(tile, jnp.float32)] + [(tile, jnp.bfloat16)] * (LINE - 1)
    kept, *sent = call(line_kernel, [VMEM] * 4, outs, 1 << 20)(own, *arrived)
    return kept, sent


def smooth_kernel(cells, before, after, smooth):
    rows, share = cells.shape
    depth = rows // 2
    z = lax.broadcasted_iota(jnp.int32, (depth, share), 0)
    for c in range(2):
        at = slice(c * depth, (c + 1) * depth)
        value = cells[at, :]
        down = jnp.where(z == 0, before[c : c + 1, :], pltpu.roll(value, 1, 0))
        up = jnp.where(z == depth - 1, after[c : c + 1, :], pltpu.roll(value, depth - 1, 0))
        smooth[at, :] = value - SMOOTHING * (2.0 * value - down - up)


def smoothed(cells, before, after):
    outs = [(cells.shape, jnp.float32)]
    return call(smooth_kernel, [VMEM] * 3, outs, 1 << 20, 4)(cells, before, after)[0]


def merge_kernel(smooth, k0, a1, a2, a3, k1, b1, b2, b3, mine, theirs, message):
    total = smooth[...] + k0[...]
    for ref in (a1, a2, a3):
        total = total + ref[...].astype(jnp.float32)
    mine[...] = total
    message[0] = total.astype(message.dtype)
    total = k1[...]
    for ref in (b1, b2, b3):
        total = total + ref[...].astype(jnp.float32)
    theirs[...] = total
    message[1] = total.astype(message.dtype)


def merged(smooth, kept, reached):
    outs = [(smooth.shape, jnp.float32)] * 2 + [((2, *smooth.shape), jnp.bfloat16)]
    return call(merge_kernel, [VMEM] * 9, outs, 1 << 20, 4)(
        smooth, kept[0], *reached[0], kept[1], *reached[1]
    )


def finish_kernel(mine, theirs, crossed, following, own, visiting):
    depth = mine.shape[0] // 2
    for c in range(2):
        at = slice(c * depth, (c + 1) * depth)
        here = mine[at, :] + crossed[1, at, :].astype(jnp.float32)
        there = theirs[at, :] + crossed[0, at, :].astype(jnp.float32)
        if c == 1:
            here, there = jnp.maximum(here, 0.0), jnp.maximum(there, 0.0)
        following[at, :] = here
        own[at, :] = here.astype(own.dtype)
        visiting[at, :] = there.astype(visiting.dtype)


def finished(mine, theirs, crossed):
    outs = [(mine.shape, jnp.float32)] + [(mine.shape, jnp.bfloat16)] * 2
    return call(finish_kernel, [VMEM] * 3, outs, 1 << 20, 4)(mine, theirs, crossed)


def projected(image, a, piece, held, j, starts):
    block = held.shape[3]
    start = pl.multiple_of(starts[a, j] * block, block)
    part = lax.dot_general(
        piece, held[a, j], (((1,), (1,)), ((), ())), preferred_element_type=jnp.float32
    )
    image[..., pl.ds(start, 2 * block)] += part


def near_kernel(table, starts, held, following, p1, p0, image, volume):
    depth = volume.shape[2]
    for c in range(2):
        volume[:, c, :] = following[c * depth : (c + 1) * depth, :].T

    def angle(a, carry):
        image[a] = jnp.zeros(image.shape[1:], image.dtype)
        for base, piece in ((place(1, 0), p1), (place(0, 0), p0)):
            for k in range(LINE):
                projected(image.at[a], a, piece[k], held, table[base + k], starts)
        return carry

    lax.fori_loop(0, image.shape[0], angle, 0)


def near(pieces, held, table, starts, following, image, volume):
    angles, _, band, block = held.shape
    flops = 2 * len(pieces) * LINE * angles * image[1] * band * block
    specs = [SMEM, SMEM] + [VMEM] * 4
    outs = [(image, jnp.float32), (volume, jnp.float32)]
    return call(near_kernel, specs, outs, flops, 16)(table, starts, held, following, *pieces)


def next_kernel(table, starts, held, before, p1, p2, p3, image):
    def angle(a, carry):
        image[a] = before[a]
        for d, piece in zip(FAR, (p1, p2, p3)):
            for k in range(LINE):
                projected(image.at[a], a, piece[k], held, table[place(0, d) + k], starts)
        return carry

    lax.fori_loop(0, image.shape[0], angle, 0)


def following_image(pieces, held, table, starts, before):
    angles, _, band, block = held.shape
    flops = 2 * len(pieces) * LINE * angles * before.shape[1] * band * block
    specs = [SMEM, SMEM] + [VMEM] * 5
    return call(next_kernel, specs, [(before.shape, jnp.float32)], flops, 16)(
        table, starts, held, before, *pieces
    )[0]


def last_kernel(table, starts, held, before, p1, p2, p3, image):
    a = pl.program_id(0)
    image[...] = before[...]
    for d, piece in zip(FAR, (p1, p2, p3)):
        for k in range(LINE):
            projected(image.at[0], a, piece[k], held, table[place(1, d) + k], starts)


def last(pieces, held, table, starts, before):
    angles, _, band, block = held.shape
    _, rows, detector = before.shape
    angle = pl.BlockSpec((1, rows, detector), lambda a: (a, 0, 0))
    return pl.pallas_call(
        last_kernel,
        grid=(angles,),
        in_specs=[SMEM, SMEM, VMEM, angle, VMEM, VMEM, VMEM],
        out_specs=angle,
        out_shape=jax.ShapeDtypeStruct(before.shape, jnp.float32),
        compiler_params=params(16),
        cost_estimate=pl.CostEstimate(
            flops=2 * len(pieces) * LINE * angles * rows * band * block,
            bytes_accessed=1 << 20,
            transcendentals=0,
        ),
        name="last",
    )(table, starts, held, before, *pieces)


def steps(updates, tiles, starts, ids, weights, volume):
    angles, _, depth, detector = updates.shape
    table = plan()
    count = lax.axis_size("slab")
    cells, head, tail = edges(volume, table)
    before = lax.ppermute(tail, "slab", [(i, i + 1) for i in range(count - 1)])
    after = lax.ppermute(head, "slab", [(i + 1, i) for i in range(count - 1)])

    arrived, own, kept, reached = {0: [], 1: []}, {}, {}, {}
    scaled = scale(updates, table, ids, weights)
    previous = scaled
    for d in FAR:
        far = back(scaled, tiles, table, starts, d, jnp.bfloat16, previous)
        previous = far[0]
        for other in (1, 0):
            arrived[other].append(moved(far[1 - other], other, True, d))
    own[1], own[0] = back(scaled, tiles, table, starts, 0, jnp.float32, previous)
    for other in (1, 0):
        kept[other], sent = line_sum(own[other], arrived[other])
        reached[other] = [moved(sent[d - 1], other, False, d) for d in FAR]
    mine, theirs, message = merged(smoothed(cells, before, after), kept, reached)
    following, lowered, visiting = finished(mine, theirs, across(message))

    lines, rest = {}, {}
    for other, block in ((0, lowered), (1, visiting)):
        came = {}
        for d in FAR:
            came[d] = moved(block, other, False, LINE - d)
        lines[other] = jnp.stack([block] + [came[d] for d in range(1, LINE)])
        rest[other] = []
        for d in FAR:
            rest[other].append(moved(lines[other], other, True, LINE - d))
    image = (angles, 2 * depth, detector)
    image, volume_next = near(
        [lines[1], lines[0]], tiles, table, starts, following, image, volume.shape
    )
    image = following_image(rest[0], tiles, table, starts, image)
    image = last(rest[1], tiles, table, starts, image)
    return volume_next, image.reshape(angles, 2, depth, detector)


def solution(mesh):
    placed = (
        P("ang", None, "slab", None),
        P("ang", None, None, None),
        P("ang", None),
        P("ang"),
        P(),
        P("ang", None, "slab"),
    )
    return jax.shard_map(
        steps,
        mesh=mesh,
        in_specs=placed,
        out_specs=(P("ang", None, "slab"), P("ang", None, "slab", None)),
        check_vma=False,
    )
```

profile of v0, /device:TPU:70, one launch (start us, length us, event | category | flops | bytes accessed | tf_op | source)
XLA Modules:
  0.0 91.9 jit_solution(4603969051470989490)
XLA Ops:
  0.7 0.7 plan.1.table
  1.4 0.9 copy-done.2
  2.3 0.7 shard_map.79.scaled.after
  2.9 0.6 slice-done
  3.5 1.4 %slice-done.1 = s8[4194304]{0:T(1024)(128)(4,1)S(1)} async-done(((s8[8388608]{0:T(1024)(128)(4,1)}), s8[4194304]{0:T(1024)(128)(4,1)S(1)}, s32[]{:S(2)}) %slice-start.1) | async-done | bytes 4194328
  4.9 1.8 %shard_map.80 = (bf16[4,256,128]{2,1,0:T(8,128)(2,1)S(1)}, bf16[4,256,128]{2,1,0:T(8,128)(2,1)S(1)}) custom-call(s32[32]{0:T(128)S(1)} %plan.1.table, s32[4,32]{1,0:T(4,128)S(1)} %copy-done.1, bf16[4,256,512]{2,1,0:T(8,128)(2,1)S(1)} %shard_map.79.scaled.after, bf16[4,32,256,128]{3,2,1,0:T(8,128)(2,1)S(1)} %bitcast.10, ...), custom_call_target="tpu_custom_call" | custom-call | flops 536870912 | bytes 1048576 | tf_op jit(solution)/shard_map/pallas_call | solution.py:145
  6.8 1.5 %collective-permute-start.2 = (bf16[4,256,128]{2,1,0:T(8,128)(2,1)S(1)}, bf16[4,256,128]{2,1,0:T(8,128)(2,1)S(1)}, u32[]{:S(2)}, u32[]{:S(2)}) collective-permute-start(bf16[4,256,128]{2,1,0:T(8,128)(2,1)S(1)} %get-tuple-element.36), channel_id=1, source_target_pairs={{0,16},{8,24},{16,0},{24,8},{32,160},{40,168},{48,176},{56,184},{6... | collective-permute-start | bytes 786440 | tf_op jit(solution)/shard_map/ppermute | solution.py:30
  8.3 1.8 %shard_map.81 = (bf16[4,256,128]{2,1,0:T(8,128)(2,1)S(1)}, bf16[4,256,128]{2,1,0:T(8,128)(2,1)S(1)}) custom-call(s32[32]{0:T(128)S(1)} %plan.1.table, s32[4,32]{1,0:T(4,128)S(1)} %copy-done.1, bf16[4,256,512]{2,1,0:T(8,128)(2,1)S(1)} %shard_map.79.scaled.after, bf16[4,32,256,128]{3,2,1,0:T(8,128)(2,1)S(1)} %bitcast.10, ...), custom_call_target="tpu_custom_call" | custom-call | flops 536870912 | bytes 1048576 | tf_op jit(solution)/shard_map/pallas_call | solution.py:145
  10.1 2.2 %collective-permute-start.3 = (bf16[4,256,128]{2,1,0:T(8,128)(2,1)S(1)}, bf16[4,256,128]{2,1,0:T(8,128)(2,1)S(1)}, u32[]{:S(2)}, u32[]{:S(2)}) collective-permute-start(bf16[4,256,128]{2,1,0:T(8,128)(2,1)S(1)} %get-tuple-element.37), channel_id=1, source_target_pairs={{0,8},{8,16},{16,24},{24,0},{32,96},{40,104},{48,112},{56,120},{64... | collective-permute-start | bytes 786440 | tf_op jit(solution)/shard_map/ppermute | solution.py:30
  12.3 1.8 %shard_map.82 = (bf16[4,256,128]{2,1,0:T(8,128)(2,1)S(1)}, bf16[4,256,128]{2,1,0:T(8,128)(2,1)S(1)}) custom-call(s32[32]{0:T(128)S(1)} %plan.1.table, s32[4,32]{1,0:T(4,128)S(1)} %copy-done.1, bf16[4,256,512]{2,1,0:T(8,128)(2,1)S(1)} %shard_map.79.scaled.after, bf16[4,32,256,128]{3,2,1,0:T(8,128)(2,1)S(1)} %bitcast.10, ...), custom_call_target="tpu_custom_call" | custom-call | flops 536870912 | bytes 1048576 | tf_op jit(solution)/shard_map/pallas_call | solution.py:145
  14.2 3.3 %collective-permute-start.8 = (bf16[4,256,128]{2,1,0:T(8,128)(2,1)S(1)}, bf16[4,256,128]{2,1,0:T(8,128)(2,1)S(1)}, u32[]{:S(2)}, u32[]{:S(2)}) collective-permute-start(bf16[4,256,128]{2,1,0:T(8,128)(2,1)S(1)} %get-tuple-element.32.after), channel_id=1, source_target_pairs={{0,128},{8,136},{16,144},{24,152},{32,48},{40,56},{48,32},{56,40},... | collective-permute-start | bytes 786440 | tf_op jit(solution)/shard_map/ppermute | solution.py:30
  17.5 0.7 collective-permute-start.9
  18.2 2.5 %collective-permute-start.10 = (bf16[4,256,128]{2,1,0:T(8,128)(2,1)S(1)}, bf16[4,256,128]{2,1,0:T(8,128)(2,1)S(1)}, u32[]{:S(2)}, u32[]{:S(2)}) collective-permute-start(bf16[4,256,128]{2,1,0:T(8,128)(2,1)S(1)} %get-tuple-element.34.after), channel_id=1, source_target_pairs={{0,192},{8,200},{16,208},{24,216},{32,56},{40,32},{48,40},{56,48},... | collective-permute-start | bytes 786440 | tf_op jit(solution)/shard_map/ppermute | solution.py:30
  20.7 1.8 %shard_map.83 = (f32[4,256,128]{2,1,0:T(8,128)S(1)}, f32[4,256,128]{2,1,0:T(8,128)S(1)}) custom-call(s32[32]{0:T(128)S(1)} %plan.1.table, s32[4,32]{1,0:T(4,128)S(1)} %copy-done.1, bf16[4,256,512]{2,1,0:T(8,128)(2,1)S(1)} %shard_map.79.scaled.after, bf16[4,32,256,128]{3,2,1,0:T(8,128)(2,1)S(1)} %bitcast.10, bf16[4,256,128]{2,1,0:T(8,128)(2,1)S(1)} %get-tuple-element.34.after), custom_call_target="tpu_custom_call" | custom-call | flops 536870912 | bytes 1048576 | tf_op jit(solution)/shard_map/pallas_call | solution.py:145
  22.6 0.3 collective-permute-done.4.s3
  22.9 0.1 shard_map.84
  23.0 3.3 %collective-permute-start.5 = (bf16[256,128]{1,0:T(8,128)(2,1)S(1)}, bf16[256,128]{1,0:T(8,128)(2,1)S(1)}, u32[]{:S(2)}, u32[]{:S(2)}) collective-permute-start(bf16[256,128]{1,0:T(8,128)(2,1)S(1)} %get-tuple-element.40), channel_id=1, source_target_pairs={{0,128},{8,136},{16,144},{24,152},{32,48},{40,56},{48,32},{56,40},... | collective-permute-start | bytes 196616 | tf_op jit(solution)/shard_map/ppermute | solution.py:30
  26.3 0.7 shard_map.77
  27.0 1.9 %collective-permute-start = (f32[2,128]{1,0:T(2,128)S(1)}, f32[2,128]{1,0:T(2,128)S(1)}, u32[]{:S(2)}, u32[]{:S(2)}) collective-permute-start(f32[2,128]{1,0:T(2,128)S(1)} %get-tuple-element.30), channel_id=1, source_target_pairs={{0,1},{1,2},{2,3},{3,4},{4,5},{5,6},{6,7},{8,9},{9,10},{10,11},{11... | collective-permute-start | bytes 3080 | tf_op jit(solution)/shard_map/ppermute | solution.py:306
  28.9 3.6 %collective-permute-start.1 = (f32[2,128]{1,0:T(2,128)S(1)}, f32[2,128]{1,0:T(2,128)S(1)}, u32[]{:S(2)}, u32[]{:S(2)}) collective-permute-start(f32[2,128]{1,0:T(2,128)S(1)} %get-tuple-element.31), channel_id=1, source_target_pairs={{1,0},{2,1},{3,2},{4,3},{5,4},{6,5},{7,6},{9,8},{10,9},{11,10},{12... | collective-permute-start | bytes 3080 | tf_op jit(solution)/shard_map/ppermute | solution.py:307
  32.6 0.8 collective-permute-start.6
  33.3 2.6 %collective-permute-start.7 = (bf16[256,128]{1,0:T(8,128)(2,1)S(1)}, bf16[256,128]{1,0:T(8,128)(2,1)S(1)}, u32[]{:S(2)}, u32[]{:S(2)}) collective-permute-start(bf16[256,128]{1,0:T(8,128)(2,1)S(1)} %get-tuple-element.42), channel_id=1, source_target_pairs={{0,192},{8,200},{16,208},{24,216},{32,56},{40,32},{48,40},{56,48},... | collective-permute-start | bytes 196616 | tf_op jit(solution)/shard_map/ppermute | solution.py:30
  36.0 0.9 collective-permute-start.11
  36.9 2.0 %collective-permute-start.12 = (bf16[256,128]{1,0:T(8,128)(2,1)S(1)}, bf16[256,128]{1,0:T(8,128)(2,1)S(1)}, u32[]{:S(2)}, u32[]{:S(2)}) collective-permute-start(bf16[256,128]{1,0:T(8,128)(2,1)S(1)} %get-tuple-element.46), channel_id=1, source_target_pairs={{0,8},{8,16},{16,24},{24,0},{32,96},{40,104},{48,112},{56,120},{64... | collective-permute-start | bytes 196616 | tf_op jit(solution)/shard_map/ppermute | solution.py:30
  39.0 3.5 %collective-permute-done.11.b1 = bf16[256,128]{1,0:T(8,128)(2,1)S(1)} collective-permute-done((bf16[256,128]{1,0:T(8,128)(2,1)S(1)}, bf16[256,128]{1,0:T(8,128)(2,1)S(1)}, u32[]{:S(2)}, u32[]{:S(2)}) %collective-permute-start.11) | collective-permute-done | bytes 65568 | tf_op jit(solution)/shard_map/ppermute | solution.py:30
  42.5 1.9 %collective-permute-done.13.b3 = bf16[256,128]{1,0:T(8,128)(2,1)S(1)} collective-permute-done((bf16[256,128]{1,0:T(8,128)(2,1)S(1)}, bf16[256,128]{1,0:T(8,128)(2,1)S(1)}, u32[]{:S(2)}, u32[]{:S(2)}) %collective-permute-start.13) | collective-permute-done | bytes 65568 | tf_op jit(solution)/shard_map/ppermute | solution.py:30
  44.5 2.5 %collective-permute-start.14 = (bf16[2,256,128]{2,1,0:T(8,128)(2,1)S(1)}, bf16[2,256,128]{2,1,0:T(8,128)(2,1)S(1)}, u32[]{:S(2)}, u32[]{:S(2)}) collective-permute-start(bf16[2,256,128]{2,1,0:T(8,128)(2,1)S(1)} %get-tuple-element.50), channel_id=1, source_target_pairs={{0,32},{8,40},{16,48},{24,56},{32,0},{40,8},{48,16},{56,24},{64,96... | collective-permute-start | bytes 393224 | tf_op jit(solution)/shard_map/ppermute | solution.py:39
  47.0 6.9 %collective-permute-done.14.crossed = bf16[2,256,128]{2,1,0:T(8,128)(2,1)S(1)} collective-permute-done((bf16[2,256,128]{2,1,0:T(8,128)(2,1)S(1)}, bf16[2,256,128]{2,1,0:T(8,128)(2,1)S(1)}, u32[]{:S(2)}, u32[]{:S(2)}) %collective-permute-start.14) | collective-permute-done | bytes 131104 | tf_op jit(solution)/shard_map/ppermute | solution.py:39
  53.9 0.5 collective-permute-start.20
  54.3 2.4 %collective-permute-start.19 = (bf16[256,128]{1,0:T(8,128)(2,1)S(1)}, bf16[256,128]{1,0:T(8,128)(2,1)S(1)}, u32[]{:S(2)}, u32[]{:S(2)}) collective-permute-start(bf16[256,128]{1,0:T(8,128)(2,1)S(1)} %get-tuple-element.53), channel_id=1, source_target_pairs={{0,128},{8,136},{16,144},{24,152},{32,48},{40,56},{48,32},{56,40},... | collective-permute-start | bytes 196616 | tf_op jit(solution)/shard_map/ppermute | solution.py:30
  56.8 0.8 collective-permute-start.18
  57.5 2.0 %collective-permute-done.20 = bf16[256,128]{1,0:T(8,128)(2,1)S(1)} collective-permute-done((bf16[256,128]{1,0:T(8,128)(2,1)S(1)}, bf16[256,128]{1,0:T(8,128)(2,1)S(1)}, u32[]{:S(2)}, u32[]{:S(2)}) %collective-permute-start.20) | collective-permute-done | bytes 65568 | tf_op jit(solution)/shard_map/ppermute | solution.py:30
  59.5 0.7 collective-permute-done.19
  60.2 0.9 collective-permute-done.18
  61.1 1.3 %collective-permute-start.21 = (bf16[4,256,128]{2,1,0:T(8,128)(2,1)S(1)}, bf16[4,256,128]{2,1,0:T(8,128)(2,1)S(1)}, u32[]{:S(2)}, u32[]{:S(2)}) collective-permute-start(bf16[4,256,128]{2,1,0:T(8,128)(2,1)S(1)} %pad_maximum_fusion.1.p0), channel_id=1, source_target_pairs={{0,16},{8,24},{16,0},{24,8},{32,160},{40,168},{48,176},{56,184},{6... | collective-permute-start | bytes 786440 | tf_op jit(solution)/shard_map/ppermute | solution.py:30
  62.4 1.9 %collective-permute-start.17 = (bf16[256,128]{1,0:T(8,128)(2,1)S(1)}, bf16[256,128]{1,0:T(8,128)(2,1)S(1)}, u32[]{:S(2)}, u32[]{:S(2)}) collective-permute-start(bf16[256,128]{1,0:T(8,128)(2,1)S(1)} %get-tuple-element.52), channel_id=1, source_target_pairs={{0,8},{8,16},{16,24},{24,0},{32,96},{40,104},{48,112},{56,120},{64... | collective-permute-start | bytes 196616 | tf_op jit(solution)/shard_map/ppermute | solution.py:30
  64.3 2.3 %collective-permute-start.16 = (bf16[256,128]{1,0:T(8,128)(2,1)S(1)}, bf16[256,128]{1,0:T(8,128)(2,1)S(1)}, u32[]{:S(2)}, u32[]{:S(2)}) collective-permute-start(bf16[256,128]{1,0:T(8,128)(2,1)S(1)} %get-tuple-element.52), channel_id=1, source_target_pairs={{0,16},{8,24},{16,0},{24,8},{32,160},{40,168},{48,176},{56,184},{6... | collective-permute-start | bytes 196616 | tf_op jit(solution)/shard_map/ppermute | solution.py:30
  66.6 1.2 %collective-permute-start.22 = (bf16[4,256,128]{2,1,0:T(8,128)(2,1)S(1)}, bf16[4,256,128]{2,1,0:T(8,128)(2,1)S(1)}, u32[]{:S(2)}, u32[]{:S(2)}) collective-permute-start(bf16[4,256,128]{2,1,0:T(8,128)(2,1)S(1)} %pad_maximum_fusion.1.p0), channel_id=1, source_target_pairs={{0,24},{8,0},{16,8},{24,16},{32,224},{40,232},{48,240},{56,248},{6... | collective-permute-start | bytes 786440 | tf_op jit(solution)/shard_map/ppermute | solution.py:30
  67.8 2.4 %collective-permute-done.17 = bf16[256,128]{1,0:T(8,128)(2,1)S(1)} collective-permute-done((bf16[256,128]{1,0:T(8,128)(2,1)S(1)}, bf16[256,128]{1,0:T(8,128)(2,1)S(1)}, u32[]{:S(2)}, u32[]{:S(2)}) %collective-permute-start.17) | collective-permute-done | bytes 65568 | tf_op jit(solution)/shard_map/ppermute | solution.py:30
  70.2 4.0 %collective-permute-start.23 = (bf16[4,256,128]{2,1,0:T(8,128)(2,1)S(1)}, bf16[4,256,128]{2,1,0:T(8,128)(2,1)S(1)}, u32[]{:S(2)}, u32[]{:S(2)}) collective-permute-start(bf16[4,256,128]{2,1,0:T(8,128)(2,1)S(1)} %pad_maximum_fusion.1.p0), channel_id=1, source_target_pairs={{0,8},{8,16},{16,24},{24,0},{32,96},{40,104},{48,112},{56,120},{64... | collective-permute-start | bytes 786440 | tf_op jit(solution)/shard_map/ppermute | solution.py:30
  74.2 1.7 %collective-permute-start.24 = (bf16[4,256,128]{2,1,0:T(8,128)(2,1)S(1)}, bf16[4,256,128]{2,1,0:T(8,128)(2,1)S(1)}, u32[]{:S(2)}, u32[]{:S(2)}) collective-permute-start(bf16[4,256,128]{2,1,0:T(8,128)(2,1)S(1)} %pad_maximum_fusion.p1), channel_id=1, source_target_pairs={{0,128},{8,136},{16,144},{24,152},{32,48},{40,56},{48,32},{56,40},... | collective-permute-start | bytes 786440 | tf_op jit(solution)/shard_map/ppermute | solution.py:30
  75.9 1.3 %collective-permute-start.25 = (bf16[4,256,128]{2,1,0:T(8,128)(2,1)S(1)}, bf16[4,256,128]{2,1,0:T(8,128)(2,1)S(1)}, u32[]{:S(2)}, u32[]{:S(2)}) collective-permute-start(bf16[4,256,128]{2,1,0:T(8,128)(2,1)S(1)} %pad_maximum_fusion.p1), channel_id=1, source_target_pairs={{0,192},{8,200},{16,208},{24,216},{32,56},{40,32},{48,40},{56,48},... | collective-permute-start | bytes 786440 | tf_op jit(solution)/shard_map/ppermute | solution.py:30
  77.2 0.7 collective-permute-start.26
  77.9 3.2 %shard_map.88 = (f32[4,256,512]{2,1,0:T(8,128)S(1)}, f32[128,2,128]{2,1,0:T(2,128)}) custom-call(s32[32]{0:T(128)S(1)} %plan.1.table, s32[4,32]{1,0:T(4,128)S(1)} %copy-done.1, bf16[4,32,256,128]{3,2,1,0:T(8,128)(2,1)S(1)} %bitcast.10, f32[256,128]{1,0:T(8,128)S(1)} %get-tuple-element.51.following, bf16[4,256,128]{2,1,0:T(8,128)(2,1)S(1)} %pad_maximum_fusion.p1, ...), custom_call_target="tpu_custom_call" | custom-call | flops 536870912 | bytes 1048576 | tf_op jit(solution)/shard_map/pallas_call | solution.py:250
  81.1 3.1 %shard_map.89.before = f32[4,256,512]{2,1,0:T(8,128)S(1)} custom-call(s32[32]{0:T(128)S(1)} %plan.1.table, s32[4,32]{1,0:T(4,128)S(1)} %copy-done.1, bf16[4,32,256,128]{3,2,1,0:T(8,128)(2,1)S(1)} %bitcast.10, f32[4,256,512]{2,1,0:T(8,128)S(1)} %get-tuple-element.55.before, bf16[4,256,128]{2,1,0:T(8,128)(2,1)S(1)} %collective-permute-done.21.p1, ...), custom_call_target="tpu_custom_call" | custom-call | flops 805306368 | bytes 1048576 | tf_op jit(solution)/shard_map/pallas_call | solution.py:268
  84.3 1.3 %collective-permute-done.25.p2 = bf16[4,256,128]{2,1,0:T(8,128)(2,1)S(1)} collective-permute-done((bf16[4,256,128]{2,1,0:T(8,128)(2,1)S(1)}, bf16[4,256,128]{2,1,0:T(8,128)(2,1)S(1)}, u32[]{:S(2)}, u32[]{:S(2)}) %collective-permute-start.25) | collective-permute-done | bytes 262176 | tf_op jit(solution)/shard_map/ppermute | solution.py:30
  85.6 2.2 %collective-permute-done.26.p3 = bf16[4,256,128]{2,1,0:T(8,128)(2,1)S(1)} collective-permute-done((bf16[4,256,128]{2,1,0:T(8,128)(2,1)S(1)}, bf16[4,256,128]{2,1,0:T(8,128)(2,1)S(1)}, u32[]{:S(2)}, u32[]{:S(2)}) %collective-permute-start.26) | collective-permute-done | bytes 262176 | tf_op jit(solution)/shard_map/ppermute | solution.py:30
  87.8 4.1 %last.1 = f32[4,256,512]{2,1,0:T(8,128)} custom-call(s32[32]{0:T(128)S(1)} %plan.1.table, s32[4,32]{1,0:T(4,128)S(1)} %copy-done.1, bf16[4,32,256,128]{3,2,1,0:T(8,128)(2,1)S(1)} %bitcast.10, f32[4,256,512]{2,1,0:T(8,128)S(1)} %shard_map.89.before, bf16[4,256,128]{2,1,0:T(8,128)(2,1)S(1)} %collective-permute-done.24.p1, ...), custom_call_target="tpu_custom_call" | custom-call | flops 805306368 | bytes 1048576 | tf_op jit(solution)/shard_map/last/pallas_call | solution.py:285
  (38 shorter events, 0.5 us)
Async XLA Ops:
  0.6 0.7 copy-start.3
  0.6 0.7 copy-start.4
  0.6 1.6 %copy-start.2 = (f32[4,2,128,512]{3,2,1,0:T(8,128)S(1)}, f32[4,2,128,512]{3,2,1,0:T(8,128)}, u32[]{:S(2)}) copy-start(f32[4,2,128,512]{3,2,1,0:T(8,128)} %updates.1) | copy-start | bytes 6291460
  0.7 2.8 %slice-start = ((s8[8388608]{0:T(1024)(128)(4,1)}), s8[4194304]{0:T(1024)(128)(4,1)S(1)}, s32[]{:S(2)}) async-start(s8[8388608]{0:T(1024)(128)(4,1)} %bitcast.9), calls=%async_computation | async-start | bytes 8388608
  2.3 2.7 %slice-start.1 = ((s8[8388608]{0:T(1024)(128)(4,1)}), s8[4194304]{0:T(1024)(128)(4,1)S(1)}, s32[]{:S(2)}) async-start(s8[8388608]{0:T(1024)(128)(4,1)} %bitcast.9), calls=%async_computation.1 | async-start | bytes 8388608
  2.3 2.7 %copy-start.1 = (s32[4,32]{1,0:T(4,128)S(1)}, s32[4,32]{1,0:T(4,128)}, u32[]{:S(2)}) copy-start(s32[4,32]{1,0:T(4,128)} %starts.13) | copy-start | bytes 1540
  6.8 11.4 %collective-permute-start.2 = (bf16[4,256,128]{2,1,0:T(8,128)(2,1)S(1)}, bf16[4,256,128]{2,1,0:T(8,128)(2,1)S(1)}, u32[]{:S(2)}, u32[]{:S(2)}) collective-permute-start(bf16[4,256,128]{2,1,0:T(8,128)(2,1)S(1)} %get-tuple-element.36), channel_id=1, source_target_pairs={{0,16},{8,24},{16,0},{24,8},{32,160},{40,168},{48,176},{56,184},{6... | collective-permute-start | bytes 786440 | tf_op jit(solution)/shard_map/ppermute | solution.py:30
  10.1 12.5 %collective-permute-start.3 = (bf16[4,256,128]{2,1,0:T(8,128)(2,1)S(1)}, bf16[4,256,128]{2,1,0:T(8,128)(2,1)S(1)}, u32[]{:S(2)}, u32[]{:S(2)}) collective-permute-start(bf16[4,256,128]{2,1,0:T(8,128)(2,1)S(1)} %get-tuple-element.37), channel_id=1, source_target_pairs={{0,8},{8,16},{16,24},{24,0},{32,96},{40,104},{48,112},{56,120},{64... | collective-permute-start | bytes 786440 | tf_op jit(solution)/shard_map/ppermute | solution.py:30
  14.1 8.8 %collective-permute-start.4 = (bf16[4,256,128]{2,1,0:T(8,128)(2,1)S(1)}, bf16[4,256,128]{2,1,0:T(8,128)(2,1)S(1)}, u32[]{:S(2)}, u32[]{:S(2)}) collective-permute-start(bf16[4,256,128]{2,1,0:T(8,128)(2,1)S(1)} %get-tuple-element.38), channel_id=1, source_target_pairs={{0,24},{8,0},{16,8},{24,16},{32,224},{40,232},{48,240},{56,248},{6... | collective-permute-start | bytes 786440 | tf_op jit(solution)/shard_map/ppermute | solution.py:30
  14.2 14.7 %collective-permute-start.8 = (bf16[4,256,128]{2,1,0:T(8,128)(2,1)S(1)}, bf16[4,256,128]{2,1,0:T(8,128)(2,1)S(1)}, u32[]{:S(2)}, u32[]{:S(2)}) collective-permute-start(bf16[4,256,128]{2,1,0:T(8,128)(2,1)S(1)} %get-tuple-element.32.after), channel_id=1, source_target_pairs={{0,128},{8,136},{16,144},{24,152},{32,48},{40,56},{48,32},{56,40},... | collective-permute-start | bytes 786440 | tf_op jit(solution)/shard_map/ppermute | solution.py:30
  17.5 15.1 %collective-permute-start.9 = (bf16[4,256,128]{2,1,0:T(8,128)(2,1)S(1)}, bf16[4,256,128]{2,1,0:T(8,128)(2,1)S(1)}, u32[]{:S(2)}, u32[]{:S(2)}) collective-permute-start(bf16[4,256,128]{2,1,0:T(8,128)(2,1)S(1)} %get-tuple-element.33.after), channel_id=1, source_target_pairs={{0,64},{8,72},{16,80},{24,88},{32,40},{40,48},{48,56},{56,32},{64,... | collective-permute-start | bytes 786440 | tf_op jit(solution)/shard_map/ppermute | solution.py:30
  18.2 8.1 %copy-start = (f32[128,2,128]{2,1,0:T(2,128)S(1)}, f32[128,2,128]{2,1,0:T(2,128)}, u32[]{:S(2)}) copy-start(f32[128,2,128]{2,1,0:T(2,128)} %volume.1) | copy-start | bytes 393220
  18.2 15.2 %collective-permute-start.10 = (bf16[4,256,128]{2,1,0:T(8,128)(2,1)S(1)}, bf16[4,256,128]{2,1,0:T(8,128)(2,1)S(1)}, u32[]{:S(2)}, u32[]{:S(2)}) collective-permute-start(bf16[4,256,128]{2,1,0:T(8,128)(2,1)S(1)} %get-tuple-element.34.after), channel_id=1, source_target_pairs={{0,192},{8,200},{16,208},{24,216},{32,56},{40,32},{48,40},{56,48},... | collective-permute-start | bytes 786440 | tf_op jit(solution)/shard_map/ppermute | solution.py:30
  23.0 15.9 %collective-permute-start.5 = (bf16[256,128]{1,0:T(8,128)(2,1)S(1)}, bf16[256,128]{1,0:T(8,128)(2,1)S(1)}, u32[]{:S(2)}, u32[]{:S(2)}) collective-permute-start(bf16[256,128]{1,0:T(8,128)(2,1)S(1)} %get-tuple-element.40), channel_id=1, source_target_pairs={{0,128},{8,136},{16,144},{24,152},{32,48},{40,56},{48,32},{56,40},... | collective-permute-start | bytes 196616 | tf_op jit(solution)/shard_map/ppermute | solution.py:30
  27.0 9.0 %collective-permute-start = (f32[2,128]{1,0:T(2,128)S(1)}, f32[2,128]{1,0:T(2,128)S(1)}, u32[]{:S(2)}, u32[]{:S(2)}) collective-permute-start(f32[2,128]{1,0:T(2,128)S(1)} %get-tuple-element.30), channel_id=1, source_target_pairs={{0,1},{1,2},{2,3},{3,4},{4,5},{5,6},{6,7},{8,9},{9,10},{10,11},{11... | collective-permute-start | bytes 3080 | tf_op jit(solution)/shard_map/ppermute | solution.py:306
  28.9 8.0 %collective-permute-start.1 = (f32[2,128]{1,0:T(2,128)S(1)}, f32[2,128]{1,0:T(2,128)S(1)}, u32[]{:S(2)}, u32[]{:S(2)}) collective-permute-start(f32[2,128]{1,0:T(2,128)S(1)} %get-tuple-element.31), channel_id=1, source_target_pairs={{1,0},{2,1},{3,2},{4,3},{5,4},{6,5},{7,6},{9,8},{10,9},{11,10},{12... | collective-permute-start | bytes 3080 | tf_op jit(solution)/shard_map/ppermute | solution.py:307
  32.6 6.4 %collective-permute-start.6 = (bf16[256,128]{1,0:T(8,128)(2,1)S(1)}, bf16[256,128]{1,0:T(8,128)(2,1)S(1)}, u32[]{:S(2)}, u32[]{:S(2)}) collective-permute-start(bf16[256,128]{1,0:T(8,128)(2,1)S(1)} %get-tuple-element.41), channel_id=1, source_target_pairs={{0,64},{8,72},{16,80},{24,88},{32,40},{40,48},{48,56},{56,32},{64,... | collective-permute-start | bytes 196616 | tf_op jit(solution)/shard_map/ppermute | solution.py:30
  33.3 5.7 %collective-permute-start.7 = (bf16[256,128]{1,0:T(8,128)(2,1)S(1)}, bf16[256,128]{1,0:T(8,128)(2,1)S(1)}, u32[]{:S(2)}, u32[]{:S(2)}) collective-permute-start(bf16[256,128]{1,0:T(8,128)(2,1)S(1)} %get-tuple-element.42), channel_id=1, source_target_pairs={{0,192},{8,200},{16,208},{24,216},{32,56},{40,32},{48,40},{56,48},... | collective-permute-start | bytes 196616 | tf_op jit(solution)/shard_map/ppermute | solution.py:30
  36.0 6.5 %collective-permute-start.11 = (bf16[256,128]{1,0:T(8,128)(2,1)S(1)}, bf16[256,128]{1,0:T(8,128)(2,1)S(1)}, u32[]{:S(2)}, u32[]{:S(2)}) collective-permute-start(bf16[256,128]{1,0:T(8,128)(2,1)S(1)} %get-tuple-element.45), channel_id=1, source_target_pairs={{0,16},{8,24},{16,0},{24,8},{32,160},{40,168},{48,176},{56,184},{6... | collective-permute-start | bytes 196616 | tf_op jit(solution)/shard_map/ppermute | solution.py:30
  36.9 5.6 %collective-permute-start.12 = (bf16[256,128]{1,0:T(8,128)(2,1)S(1)}, bf16[256,128]{1,0:T(8,128)(2,1)S(1)}, u32[]{:S(2)}, u32[]{:S(2)}) collective-permute-start(bf16[256,128]{1,0:T(8,128)(2,1)S(1)} %get-tuple-element.46), channel_id=1, source_target_pairs={{0,8},{8,16},{16,24},{24,0},{32,96},{40,104},{48,112},{56,120},{64... | collective-permute-start | bytes 196616 | tf_op jit(solution)/shard_map/ppermute | solution.py:30
  39.0 5.5 %collective-permute-start.13 = (bf16[256,128]{1,0:T(8,128)(2,1)S(1)}, bf16[256,128]{1,0:T(8,128)(2,1)S(1)}, u32[]{:S(2)}, u32[]{:S(2)}) collective-permute-start(bf16[256,128]{1,0:T(8,128)(2,1)S(1)} %get-tuple-element.47), channel_id=1, source_target_pairs={{0,24},{8,0},{16,8},{24,16},{32,224},{40,232},{48,240},{56,248},{6... | collective-permute-start | bytes 196616 | tf_op jit(solution)/shard_map/ppermute | solution.py:30
  44.5 9.3 %collective-permute-start.14 = (bf16[2,256,128]{2,1,0:T(8,128)(2,1)S(1)}, bf16[2,256,128]{2,1,0:T(8,128)(2,1)S(1)}, u32[]{:S(2)}, u32[]{:S(2)}) collective-permute-start(bf16[2,256,128]{2,1,0:T(8,128)(2,1)S(1)} %get-tuple-element.50), channel_id=1, source_target_pairs={{0,32},{8,40},{16,48},{24,56},{32,0},{40,8},{48,16},{56,24},{64,96... | collective-permute-start | bytes 393224 | tf_op jit(solution)/shard_map/ppermute | solution.py:39
  53.9 5.6 %collective-permute-start.20 = (bf16[256,128]{1,0:T(8,128)(2,1)S(1)}, bf16[256,128]{1,0:T(8,128)(2,1)S(1)}, u32[]{:S(2)}, u32[]{:S(2)}) collective-permute-start(bf16[256,128]{1,0:T(8,128)(2,1)S(1)} %get-tuple-element.53), channel_id=1, source_target_pairs={{0,64},{8,72},{16,80},{24,88},{32,40},{40,48},{48,56},{56,32},{64,... | collective-permute-start | bytes 196616 | tf_op jit(solution)/shard_map/ppermute | solution.py:30
  54.3 5.8 %collective-permute-start.19 = (bf16[256,128]{1,0:T(8,128)(2,1)S(1)}, bf16[256,128]{1,0:T(8,128)(2,1)S(1)}, u32[]{:S(2)}, u32[]{:S(2)}) collective-permute-start(bf16[256,128]{1,0:T(8,128)(2,1)S(1)} %get-tuple-element.53), channel_id=1, source_target_pairs={{0,128},{8,136},{16,144},{24,152},{32,48},{40,56},{48,32},{56,40},... | collective-permute-start | bytes 196616 | tf_op jit(solution)/shard_map/ppermute | solution.py:30
  56.8 4.3 %collective-permute-start.18 = (bf16[256,128]{1,0:T(8,128)(2,1)S(1)}, bf16[256,128]{1,0:T(8,128)(2,1)S(1)}, u32[]{:S(2)}, u32[]{:S(2)}) collective-permute-start(bf16[256,128]{1,0:T(8,128)(2,1)S(1)} %get-tuple-element.53), channel_id=1, source_target_pairs={{0,192},{8,200},{16,208},{24,216},{32,56},{40,32},{48,40},{56,48},... | collective-permute-start | bytes 196616 | tf_op jit(solution)/shard_map/ppermute | solution.py:30
  61.1 16.2 %collective-permute-start.21 = (bf16[4,256,128]{2,1,0:T(8,128)(2,1)S(1)}, bf16[4,256,128]{2,1,0:T(8,128)(2,1)S(1)}, u32[]{:S(2)}, u32[]{:S(2)}) collective-permute-start(bf16[4,256,128]{2,1,0:T(8,128)(2,1)S(1)} %pad_maximum_fusion.1.p0), channel_id=1, source_target_pairs={{0,16},{8,24},{16,0},{24,8},{32,160},{40,168},{48,176},{56,184},{6... | collective-permute-start | bytes 786440 | tf_op jit(solution)/shard_map/ppermute | solution.py:30
  62.4 7.8 %collective-permute-start.17 = (bf16[256,128]{1,0:T(8,128)(2,1)S(1)}, bf16[256,128]{1,0:T(8,128)(2,1)S(1)}, u32[]{:S(2)}, u32[]{:S(2)}) collective-permute-start(bf16[256,128]{1,0:T(8,128)(2,1)S(1)} %get-tuple-element.52), channel_id=1, source_target_pairs={{0,8},{8,16},{16,24},{24,0},{32,96},{40,104},{48,112},{56,120},{64... | collective-permute-start | bytes 196616 | tf_op jit(solution)/shard_map/ppermute | solution.py:30
  64.3 9.9 %collective-permute-start.16 = (bf16[256,128]{1,0:T(8,128)(2,1)S(1)}, bf16[256,128]{1,0:T(8,128)(2,1)S(1)}, u32[]{:S(2)}, u32[]{:S(2)}) collective-permute-start(bf16[256,128]{1,0:T(8,128)(2,1)S(1)} %get-tuple-element.52), channel_id=1, source_target_pairs={{0,16},{8,24},{16,0},{24,8},{32,160},{40,168},{48,176},{56,184},{6... | collective-permute-start | bytes 196616 | tf_op jit(solution)/shard_map/ppermute | solution.py:30
  66.6 7.6 %collective-permute-start.15 = (bf16[256,128]{1,0:T(8,128)(2,1)S(1)}, bf16[256,128]{1,0:T(8,128)(2,1)S(1)}, u32[]{:S(2)}, u32[]{:S(2)}) collective-permute-start(bf16[256,128]{1,0:T(8,128)(2,1)S(1)} %get-tuple-element.52), channel_id=1, source_target_pairs={{0,24},{8,0},{16,8},{24,16},{32,224},{40,232},{48,240},{56,248},{6... | collective-permute-start | bytes 196616 | tf_op jit(solution)/shard_map/ppermute | solution.py:30
  66.6 14.6 %collective-permute-start.22 = (bf16[4,256,128]{2,1,0:T(8,128)(2,1)S(1)}, bf16[4,256,128]{2,1,0:T(8,128)(2,1)S(1)}, u32[]{:S(2)}, u32[]{:S(2)}) collective-permute-start(bf16[4,256,128]{2,1,0:T(8,128)(2,1)S(1)} %pad_maximum_fusion.1.p0), channel_id=1, source_target_pairs={{0,24},{8,0},{16,8},{24,16},{32,224},{40,232},{48,240},{56,248},{6... | collective-permute-start | bytes 786440 | tf_op jit(solution)/shard_map/ppermute | solution.py:30
  70.2 11.0 %collective-permute-start.23 = (bf16[4,256,128]{2,1,0:T(8,128)(2,1)S(1)}, bf16[4,256,128]{2,1,0:T(8,128)(2,1)S(1)}, u32[]{:S(2)}, u32[]{:S(2)}) collective-permute-start(bf16[4,256,128]{2,1,0:T(8,128)(2,1)S(1)} %pad_maximum_fusion.1.p0), channel_id=1, source_target_pairs={{0,8},{8,16},{16,24},{24,0},{32,96},{40,104},{48,112},{56,120},{64... | collective-permute-start | bytes 786440 | tf_op jit(solution)/shard_map/ppermute | solution.py:30
  74.2 10.1 %collective-permute-start.24 = (bf16[4,256,128]{2,1,0:T(8,128)(2,1)S(1)}, bf16[4,256,128]{2,1,0:T(8,128)(2,1)S(1)}, u32[]{:S(2)}, u32[]{:S(2)}) collective-permute-start(bf16[4,256,128]{2,1,0:T(8,128)(2,1)S(1)} %pad_maximum_fusion.p1), channel_id=1, source_target_pairs={{0,128},{8,136},{16,144},{24,152},{32,48},{40,56},{48,32},{56,40},... | collective-permute-start | bytes 786440 | tf_op jit(solution)/shard_map/ppermute | solution.py:30
  75.9 9.7 %collective-permute-start.25 = (bf16[4,256,128]{2,1,0:T(8,128)(2,1)S(1)}, bf16[4,256,128]{2,1,0:T(8,128)(2,1)S(1)}, u32[]{:S(2)}, u32[]{:S(2)}) collective-permute-start(bf16[4,256,128]{2,1,0:T(8,128)(2,1)S(1)} %pad_maximum_fusion.p1), channel_id=1, source_target_pairs={{0,192},{8,200},{16,208},{24,216},{32,56},{40,32},{48,40},{56,48},... | collective-permute-start | bytes 786440 | tf_op jit(solution)/shard_map/ppermute | solution.py:30
  77.2 10.5 %collective-permute-start.26 = (bf16[4,256,128]{2,1,0:T(8,128)(2,1)S(1)}, bf16[4,256,128]{2,1,0:T(8,128)(2,1)S(1)}, u32[]{:S(2)}, u32[]{:S(2)}) collective-permute-start(bf16[4,256,128]{2,1,0:T(8,128)(2,1)S(1)} %pad_maximum_fusion.p1), channel_id=1, source_target_pairs={{0,64},{8,72},{16,80},{24,88},{32,40},{40,48},{48,56},{56,32},{64,... | collective-permute-start | bytes 786440 | tf_op jit(solution)/shard_map/ppermute | solution.py:30
where the time goes:
time: 92.1 us; the launch traced here: 91.9 us
  starting transfers between devices  45.8 us (50%)
  waiting for transfers between devices  22 us (24%)
  Pallas kernels  20.2 us (22%)
  local copies, waits for them, and re-layouts  2.9 us (3%)
    ppermute x24, starting transfers between devices, moved(): return lax.ppermute(value, 'ang', moves(other, first, delta))  37.8 us
    ppermute x24, waiting for transfers between devices, moved(): return lax.ppermute(value, 'ang', moves(other, first, delta))  15.2 us
    pallas_call x4, Pallas kernels, back(): return call(kernel, specs, outs, flops)(table, starts, scaled, held, after)  7.31 us
    ppermute x1, waiting for transfers between devices, across(): return lax.ppermute(value, 'ang', half)  6.85 us
    pallas_call x1, Pallas kernels, last(): pl.pallas_call(last_kernel, grid=(angles,), in_specs=[SMEM, SMEM, VMEM, a...  4.14 us
    ppermute x1, starting transfers between devices, steps(): after = lax.ppermute(head, 'slab', [(i + 1, i) for i in range(count - 1)])  3.64 us
    pallas_call x1, Pallas kernels, near(): call(near_kernel, specs, outs, flops, 16)  3.21 us
    pallas_call x1, Pallas kernels, following_image(): call(next_kernel, specs, [(before.shape, jnp.float32)], flops, 16)  3.13 us
  transfers between devices with their start and end apart: 27, of which 10 were waited for; matrix products, arithmetic and copies ran while one was open for 0% of the time, Pallas kernels for 14%

commit v1 on v0

--- a/solution.py
+++ b/solution.py
@@ -218,84 +218,93 @@
     return call(finish_kernel, [VMEM] * 3, outs, 1 << 20, 4)(mine, theirs, crossed)
 
 
-def projected(image, a, piece, held, j, starts):
-    block = held.shape[3]
-    start = pl.multiple_of(starts[a, j] * block, block)
-    part = lax.dot_general(
-        piece, held[a, j], (((1,), (1,)), ((), ())), preferred_element_type=jnp.float32
-    )
-    image[..., pl.ds(start, 2 * block)] += part
-
-
-def near_kernel(table, starts, held, following, p1, p0, image, volume):
+NEAR = ((1, 0), (0, 0))
+NEXT = tuple((0, d) for d in FAR)
+LAST = tuple((1, d) for d in FAR)
+
+
+def spread_kernel(table, starts, tiles, after, *outs):
+    block = tiles.shape[3]
+    zeros = jnp.zeros((block, block), tiles.dtype)
+
+    def angle(a, carry):
+        for out, groups in zip(outs, (NEAR, NEXT, LAST)):
+            for g, (other, d) in enumerate(groups):
+                for k in range(LINE):
+                    j = table[place(other, d) + k]
+                    first = starts[a, j]
+                    column = slice((g * LINE + k) * block, (g * LINE + k + 1) * block)
+                    for empty in (jnp.where(first == 0, 2, 0), jnp.where(first == 2, 1, 3)):
+                        at = pl.ds(pl.multiple_of(empty * block, block), block)
+                        out[a, at, column] = zeros
+                    at = pl.ds(pl.multiple_of(first * block, block), 2 * block)
+                    out[a, at, column] = tiles[a, j]
+        return carry
+
+    lax.fori_loop(0, tiles.shape[0], angle, 0)
+
+
+def spread(tiles, table, starts, detector, after):
+    angles, _, _, block = tiles.shape
+    outs = [
+        ((angles, detector, len(groups) * LINE * block), tiles.dtype)
+        for groups in (NEAR, NEXT, LAST)
+    ]
+    specs = [SMEM, SMEM, VMEM, pl.BlockSpec(memory_space=pl.ANY)]
+    return call(spread_kernel, specs, outs, 1 << 31, 16)(table, starts, tiles, after)
+
+
+def projected(pieces, weights):
+    row = jnp.concatenate([piece[k] for piece in pieces for k in range(LINE)], axis=1)
+    return lax.dot_general(
+        row, weights, (((1,), (1,)), ((), ())), preferred_element_type=jnp.float32
+    )
+
+
+def near_kernel(weights, following, p1, p0, image, volume):
     depth = volume.shape[2]
     for c in range(2):
         volume[:, c, :] = following[c * depth : (c + 1) * depth, :].T
-
-    def angle(a, carry):
-        image[a] = jnp.zeros(image.shape[1:], image.dtype)
-        for base, piece in ((place(1, 0), p1), (place(0, 0), p0)):
-            for k in range(LINE):
-                projected(image.at[a], a, piece[k], held, table[base + k], starts)
-        return carry
-
-    lax.fori_loop(0, image.shape[0], angle, 0)
-
-
-def near(pieces, held, table, starts, following, image, volume):
-    angles, _, band, block = held.shape
-    flops = 2 * len(pieces) * LINE * angles * image[1] * band * block
-    specs = [SMEM, SMEM] + [VMEM] * 4
+    for a in range(image.shape[0]):
+        image[a] = projected((p1, p0), weights[a])
+
+
+def near(pieces, weights, following, image, volume):
     outs = [(image, jnp.float32), (volume, jnp.float32)]
-    return call(near_kernel, specs, outs, flops, 16)(table, starts, held, following, *pieces)
-
-
-def next_kernel(table, starts, held, before, p1, p2, p3, image):
-    def angle(a, carry):
-        image[a] = before[a]
-        for d, piece in zip(FAR, (p1, p2, p3)):
-            for k in range(LINE):
-                projected(image.at[a], a, piece[k], held, table[place(0, d) + k], starts)
-        return carry
-
-    lax.fori_loop(0, image.shape[0], angle, 0)
-
-
-def following_image(pieces, held, table, starts, before):
-    angles, _, band, block = held.shape
-    flops = 2 * len(pieces) * LINE * angles * before.shape[1] * band * block
-    specs = [SMEM, SMEM] + [VMEM] * 5
-    return call(next_kernel, specs, [(before.shape, jnp.float32)], flops, 16)(
-        table, starts, held, before, *pieces
-    )[0]
-
-
-def last_kernel(table, starts, held, before, p1, p2, p3, image):
+    flops = 2 * weights.size * image[1]
+    return call(near_kernel, [VMEM] * 4, outs, flops, 16)(weights, following, *pieces)
+
+
+def next_kernel(weights, before, p1, p2, p3, image):
+    for a in range(image.shape[0]):
+        image[a] = before[a] + projected((p1, p2, p3), weights[a])
+
+
+def further(pieces, weights, before):
+    outs = [(before.shape, jnp.float32)]
+    flops = 2 * weights.size * before.shape[1]
+    return call(next_kernel, [VMEM] * 5, outs, flops, 16)(weights, before, *pieces)[0]
+
+
+def last_kernel(weights, before, p1, p2, p3, image):
     a = pl.program_id(0)
-    image[...] = before[...]
-    for d, piece in zip(FAR, (p1, p2, p3)):
-        for k in range(LINE):
-            projected(image.at[0], a, piece[k], held, table[place(1, d) + k], starts)
-
-
-def last(pieces, held, table, starts, before):
-    angles, _, band, block = held.shape
-    _, rows, detector = before.shape
-    angle = pl.BlockSpec((1, rows, detector), lambda a: (a, 0, 0))
+    image[0] = before[a] + projected((p1, p2, p3), weights[a])
+
+
+def last(pieces, weights, before):
+    angles, rows, detector = before.shape
     return pl.pallas_call(
         last_kernel,
         grid=(angles,),
-        in_specs=[SMEM, SMEM, VMEM, angle, VMEM, VMEM, VMEM],
-        out_specs=angle,
+        in_specs=[VMEM] * 5,
+        out_specs=pl.BlockSpec((1, rows, detector), lambda a: (a, 0, 0)),
         out_shape=jax.ShapeDtypeStruct(before.shape, jnp.float32),
         compiler_params=params(16),
         cost_estimate=pl.CostEstimate(
-            flops=2 * len(pieces) * LINE * angles * rows * band * block,
-            bytes_accessed=1 << 20,
-            transcendentals=0,
+            flops=2 * weights.size * rows, bytes_accessed=1 << 20, transcendentals=0
         ),
         name="last",
-    )(table, starts, held, before, *pieces)
+    )(weights, before, *pieces)
 
 
 def steps(updates, tiles, starts, ids, weights, volume):
@@ -319,7 +328,9 @@
         kept[other], sent = line_sum(own[other], arrived[other])
         reached[other] = [moved(sent[d - 1], other, False, d) for d in FAR]
     mine, theirs, message = merged(smoothed(cells, before, after), kept, reached)
-    following, lowered, visiting = finished(mine, theirs, across(message))
+    crossed = across(message)
+    weights = spread(tiles, table, starts, detector, message)
+    following, lowered, visiting = finished(mine, theirs, crossed)
 
     lines, rest = {}, {}
     for other, block in ((0, lowered), (1, visiting)):
@@ -331,11 +342,9 @@
         for d in FAR:
             rest[other].append(moved(lines[other], other, True, LINE - d))
     image = (angles, 2 * depth, detector)
-    image, volume_next = near(
-        [lines[1], lines[0]], tiles, table, starts, following, image, volume.shape
-    )
-    image = following_image(rest[0], tiles, table, starts, image)
-    image = last(rest[1], tiles, table, starts, image)
+    image, volume_next = near([lines[1], lines[0]], weights[0], following, image, volume.shape)
+    image = further(rest[0], weights[1], image)
+    image = last(rest[1], weights[2], image)
     return volume_next, image.reshape(angles, 2, depth, detector)
 
 

time: 92.1 us -> 96.6 us (1.049)
  the two profiles are of different devices: /device:TPU:70 before, /device:TPU:2 now
where the time goes in v1:
time: 96.6 us; the launch traced here: 96.3 us
  starting transfers between devices  42.7 us (44%)
  waiting for transfers between devices  29.3 us (30%)
  Pallas kernels  20.5 us (21%)
  local copies, waits for them, and re-layouts  2.9 us (3%)
    ppermute x24, starting transfers between devices, moved(): return lax.ppermute(value, 'ang', moves(other, first, delta))  33 us
    ppermute x24, waiting for transfers between devices, moved(): return lax.ppermute(value, 'ang', moves(other, first, delta))  24.6 us
    pallas_call x4, Pallas kernels, back(): return call(kernel, specs, outs, flops)(table, starts, scaled, held, after)  7.3 us
    ppermute x1, starting transfers between devices, across(): return lax.ppermute(value, 'ang', half)  7.13 us
    ppermute x1, waiting for transfers between devices, across(): return lax.ppermute(value, 'ang', half)  3.94 us
    pallas_call x1, Pallas kernels, spread(): call(spread_kernel, specs, outs, 1 << 31, 16)(table, starts, tiles, after)  3.6 us
    pallas_call x1, Pallas kernels, last(): pl.pallas_call(last_kernel, grid=(angles,), in_specs=[VMEM] * 5, out_spec...  3.41 us
    unnamed x14, local copies, waits for them, and re-layouts  2.9 us
  transfers between devices with their start and end apart: 27, of which 13 were waited for; matrix products, arithmetic and copies ran while one was open for 0% of the time, Pallas kernels for 11%

profile of v1, /device:TPU:2, one launch (start us, length us, event | category | flops | bytes accessed | tf_op | source)
XLA Modules:
  0.0 96.3 jit_solution(5663894048168274719)
XLA Ops:
  0.7 0.7 plan.1.table
  1.4 0.9 copy-done.2
  2.2 0.7 shard_map.79.scaled.after
  3.5 1.4 %slice-done.1 = s8[4194304]{0:T(1024)(128)(4,1)S(1)} async-done(((s8[8388608]{0:T(1024)(128)(4,1)}), s8[4194304]{0:T(1024)(128)(4,1)S(1)}, s32[]{:S(2)}) %slice-start.1) | async-done | bytes 4194328
  4.9 1.8 %shard_map.80 = (bf16[4,256,128]{2,1,0:T(8,128)(2,1)S(1)}, bf16[4,256,128]{2,1,0:T(8,128)(2,1)S(1)}) custom-call(s32[32]{0:T(128)S(1)} %plan.1.table, s32[4,32]{1,0:T(4,128)S(1)} %copy-done.1, bf16[4,256,512]{2,1,0:T(8,128)(2,1)S(1)} %shard_map.79.scaled.after, bf16[4,32,256,128]{3,2,1,0:T(8,128)(2,1)S(1)} %bitcast.10, ...), custom_call_target="tpu_custom_call" | custom-call | flops 536870912 | bytes 1048576 | tf_op jit(solution)/shard_map/pallas_call | solution.py:145
  6.8 1.8 %shard_map.81 = (bf16[4,256,128]{2,1,0:T(8,128)(2,1)S(1)}, bf16[4,256,128]{2,1,0:T(8,128)(2,1)S(1)}) custom-call(s32[32]{0:T(128)S(1)} %plan.1.table, s32[4,32]{1,0:T(4,128)S(1)} %copy-done.1, bf16[4,256,512]{2,1,0:T(8,128)(2,1)S(1)} %shard_map.79.scaled.after, bf16[4,32,256,128]{3,2,1,0:T(8,128)(2,1)S(1)} %bitcast.10, ...), custom_call_target="tpu_custom_call" | custom-call | flops 536870912 | bytes 1048576 | tf_op jit(solution)/shard_map/pallas_call | solution.py:145
  8.6 1.8 %shard_map.82 = (bf16[4,256,128]{2,1,0:T(8,128)(2,1)S(1)}, bf16[4,256,128]{2,1,0:T(8,128)(2,1)S(1)}) custom-call(s32[32]{0:T(128)S(1)} %plan.1.table, s32[4,32]{1,0:T(4,128)S(1)} %copy-done.1, bf16[4,256,512]{2,1,0:T(8,128)(2,1)S(1)} %shard_map.79.scaled.after, bf16[4,32,256,128]{3,2,1,0:T(8,128)(2,1)S(1)} %bitcast.10, ...), custom_call_target="tpu_custom_call" | custom-call | flops 536870912 | bytes 1048576 | tf_op jit(solution)/shard_map/pallas_call | solution.py:145
  10.4 3.1 %collective-permute-start.10 = (bf16[4,256,128]{2,1,0:T(8,128)(2,1)S(1)}, bf16[4,256,128]{2,1,0:T(8,128)(2,1)S(1)}, u32[]{:S(2)}, u32[]{:S(2)}) collective-permute-start(bf16[4,256,128]{2,1,0:T(8,128)(2,1)S(1)} %get-tuple-element.37.after), channel_id=1, source_target_pairs={{0,192},{8,200},{16,208},{24,216},{32,56},{40,32},{48,40},{56,48},... | collective-permute-start | bytes 786440 | tf_op jit(solution)/shard_map/ppermute | solution.py:30
  13.5 2.2 %collective-permute-start.8 = (bf16[4,256,128]{2,1,0:T(8,128)(2,1)S(1)}, bf16[4,256,128]{2,1,0:T(8,128)(2,1)S(1)}, u32[]{:S(2)}, u32[]{:S(2)}) collective-permute-start(bf16[4,256,128]{2,1,0:T(8,128)(2,1)S(1)} %get-tuple-element.35.after), channel_id=1, source_target_pairs={{0,128},{8,136},{16,144},{24,152},{32,48},{40,56},{48,32},{56,40},... | collective-permute-start | bytes 786440 | tf_op jit(solution)/shard_map/ppermute | solution.py:30
  16.3 1.5 %collective-permute-start.3 = (bf16[4,256,128]{2,1,0:T(8,128)(2,1)S(1)}, bf16[4,256,128]{2,1,0:T(8,128)(2,1)S(1)}, u32[]{:S(2)}, u32[]{:S(2)}) collective-permute-start(bf16[4,256,128]{2,1,0:T(8,128)(2,1)S(1)} %get-tuple-element.40), channel_id=1, source_target_pairs={{0,8},{8,16},{16,24},{24,0},{32,96},{40,104},{48,112},{56,120},{64... | collective-permute-start | bytes 786440 | tf_op jit(solution)/shard_map/ppermute | solution.py:30
  17.8 7.0 %collective-permute-done.10.s3 = bf16[4,256,128]{2,1,0:T(8,128)(2,1)S(1)} collective-permute-done((bf16[4,256,128]{2,1,0:T(8,128)(2,1)S(1)}, bf16[4,256,128]{2,1,0:T(8,128)(2,1)S(1)}, u32[]{:S(2)}, u32[]{:S(2)}) %collective-permute-start.10) | collective-permute-done | bytes 262176 | tf_op jit(solution)/shard_map/ppermute | solution.py:30
  24.7 2.1 %collective-permute-start.2 = (bf16[4,256,128]{2,1,0:T(8,128)(2,1)S(1)}, bf16[4,256,128]{2,1,0:T(8,128)(2,1)S(1)}, u32[]{:S(2)}, u32[]{:S(2)}) collective-permute-start(bf16[4,256,128]{2,1,0:T(8,128)(2,1)S(1)} %get-tuple-element.39), channel_id=1, source_target_pairs={{0,16},{8,24},{16,0},{24,8},{32,160},{40,168},{48,176},{56,184},{6... | collective-permute-start | bytes 786440 | tf_op jit(solution)/shard_map/ppermute | solution.py:30
  26.8 1.8 %shard_map.83 = (f32[4,256,128]{2,1,0:T(8,128)S(1)}, f32[4,256,128]{2,1,0:T(8,128)S(1)}) custom-call(s32[32]{0:T(128)S(1)} %plan.1.table, s32[4,32]{1,0:T(4,128)S(1)} %copy-done.1, bf16[4,256,512]{2,1,0:T(8,128)(2,1)S(1)} %shard_map.79.scaled.after, bf16[4,32,256,128]{3,2,1,0:T(8,128)(2,1)S(1)} %bitcast.10, bf16[4,256,128]{2,1,0:T(8,128)(2,1)S(1)} %get-tuple-element.37.after), custom_call_target="tpu_custom_call" | custom-call | flops 536870912 | bytes 1048576 | tf_op jit(solution)/shard_map/pallas_call | solution.py:145
  28.8 1.6 %collective-permute-start.11 = (bf16[256,128]{1,0:T(8,128)(2,1)S(1)}, bf16[256,128]{1,0:T(8,128)(2,1)S(1)}, u32[]{:S(2)}, u32[]{:S(2)}) collective-permute-start(bf16[256,128]{1,0:T(8,128)(2,1)S(1)} %get-tuple-element.48), channel_id=1, source_target_pairs={{0,16},{8,24},{16,0},{24,8},{32,160},{40,168},{48,176},{56,184},{6... | collective-permute-start | bytes 196616 | tf_op jit(solution)/shard_map/ppermute | solution.py:30
  30.5 0.7 shard_map.77
  31.1 1.3 %collective-permute-start = (f32[2,128]{1,0:T(2,128)S(1)}, f32[2,128]{1,0:T(2,128)S(1)}, u32[]{:S(2)}, u32[]{:S(2)}) collective-permute-start(f32[2,128]{1,0:T(2,128)S(1)} %get-tuple-element.33), channel_id=1, source_target_pairs={{0,1},{1,2},{2,3},{3,4},{4,5},{5,6},{6,7},{8,9},{9,10},{10,11},{11... | collective-permute-start | bytes 3080 | tf_op jit(solution)/shard_map/ppermute | solution.py:315
  32.5 1.3 %collective-permute-start.1 = (f32[2,128]{1,0:T(2,128)S(1)}, f32[2,128]{1,0:T(2,128)S(1)}, u32[]{:S(2)}, u32[]{:S(2)}) collective-permute-start(f32[2,128]{1,0:T(2,128)S(1)} %get-tuple-element.34), channel_id=1, source_target_pairs={{1,0},{2,1},{3,2},{4,3},{5,4},{6,5},{7,6},{9,8},{10,9},{11,10},{12... | collective-permute-start | bytes 3080 | tf_op jit(solution)/shard_map/ppermute | solution.py:316
  33.8 1.4 %collective-permute-start.12 = (bf16[256,128]{1,0:T(8,128)(2,1)S(1)}, bf16[256,128]{1,0:T(8,128)(2,1)S(1)}, u32[]{:S(2)}, u32[]{:S(2)}) collective-permute-start(bf16[256,128]{1,0:T(8,128)(2,1)S(1)} %get-tuple-element.49), channel_id=1, source_target_pairs={{0,8},{8,16},{16,24},{24,0},{32,96},{40,104},{48,112},{56,120},{64... | collective-permute-start | bytes 196616 | tf_op jit(solution)/shard_map/ppermute | solution.py:30
  35.2 0.7 collective-permute-start.13
  36.0 0.8 collective-permute-start.5
  36.8 0.8 collective-permute-done.1.after
  37.7 3.0 %collective-permute-start.6 = (bf16[256,128]{1,0:T(8,128)(2,1)S(1)}, bf16[256,128]{1,0:T(8,128)(2,1)S(1)}, u32[]{:S(2)}, u32[]{:S(2)}) collective-permute-start(bf16[256,128]{1,0:T(8,128)(2,1)S(1)} %get-tuple-element.44), channel_id=1, source_target_pairs={{0,64},{8,72},{16,80},{24,88},{32,40},{40,48},{48,56},{56,32},{64,... | collective-permute-start | bytes 196616 | tf_op jit(solution)/shard_map/ppermute | solution.py:30
  41.3 0.8 collective-permute-done.5.a1
  42.0 2.1 %collective-permute-done.6.a2 = bf16[256,128]{1,0:T(8,128)(2,1)S(1)} collective-permute-done((bf16[256,128]{1,0:T(8,128)(2,1)S(1)}, bf16[256,128]{1,0:T(8,128)(2,1)S(1)}, u32[]{:S(2)}, u32[]{:S(2)}) %collective-permute-start.6) | collective-permute-done | bytes 65568 | tf_op jit(solution)/shard_map/ppermute | solution.py:30
  44.1 1.2 %collective-permute-done.7.a3 = bf16[256,128]{1,0:T(8,128)(2,1)S(1)} collective-permute-done((bf16[256,128]{1,0:T(8,128)(2,1)S(1)}, bf16[256,128]{1,0:T(8,128)(2,1)S(1)}, u32[]{:S(2)}, u32[]{:S(2)}) %collective-permute-start.7) | collective-permute-done | bytes 65568 | tf_op jit(solution)/shard_map/ppermute | solution.py:30
  45.4 7.1 %collective-permute-start.14 = (bf16[2,256,128]{2,1,0:T(8,128)(2,1)S(1)}, bf16[2,256,128]{2,1,0:T(8,128)(2,1)S(1)}, u32[]{:S(2)}, u32[]{:S(2)}) collective-permute-start(bf16[2,256,128]{2,1,0:T(8,128)(2,1)S(1)} %get-tuple-element.51.after), channel_id=1, source_target_pairs={{0,32},{8,40},{16,48},{24,56},{32,0},{40,8},{48,16},{56,24},{64,96... | collective-permute-start | bytes 393224 | tf_op jit(solution)/shard_map/ppermute | solution.py:39
  52.6 3.9 %collective-permute-done.14.crossed = bf16[2,256,128]{2,1,0:T(8,128)(2,1)S(1)} collective-permute-done((bf16[2,256,128]{2,1,0:T(8,128)(2,1)S(1)}, bf16[2,256,128]{2,1,0:T(8,128)(2,1)S(1)}, u32[]{:S(2)}, u32[]{:S(2)}) %collective-permute-start.14) | collective-permute-done | bytes 131104 | tf_op jit(solution)/shard_map/ppermute | solution.py:39
  56.5 1.5 %collective-permute-start.18 = (bf16[256,128]{1,0:T(8,128)(2,1)S(1)}, bf16[256,128]{1,0:T(8,128)(2,1)S(1)}, u32[]{:S(2)}, u32[]{:S(2)}) collective-permute-start(bf16[256,128]{1,0:T(8,128)(2,1)S(1)} %get-tuple-element.57), channel_id=1, source_target_pairs={{0,192},{8,200},{16,208},{24,216},{32,56},{40,32},{48,40},{56,48},... | collective-permute-start | bytes 196616 | tf_op jit(solution)/shard_map/ppermute | solution.py:30
  58.7 1.0 %collective-permute-start.20 = (bf16[256,128]{1,0:T(8,128)(2,1)S(1)}, bf16[256,128]{1,0:T(8,128)(2,1)S(1)}, u32[]{:S(2)}, u32[]{:S(2)}) collective-permute-start(bf16[256,128]{1,0:T(8,128)(2,1)S(1)} %get-tuple-element.57), channel_id=1, source_target_pairs={{0,64},{8,72},{16,80},{24,88},{32,40},{40,48},{48,56},{56,32},{64,... | collective-permute-start | bytes 196616 | tf_op jit(solution)/shard_map/ppermute | solution.py:30
  59.7 1.4 %collective-permute-done.18 = bf16[256,128]{1,0:T(8,128)(2,1)S(1)} collective-permute-done((bf16[256,128]{1,0:T(8,128)(2,1)S(1)}, bf16[256,128]{1,0:T(8,128)(2,1)S(1)}, u32[]{:S(2)}, u32[]{:S(2)}) %collective-permute-start.18) | collective-permute-done | bytes 65568 | tf_op jit(solution)/shard_map/ppermute | solution.py:30
  61.1 2.7 %collective-permute-done.19 = bf16[256,128]{1,0:T(8,128)(2,1)S(1)} collective-permute-done((bf16[256,128]{1,0:T(8,128)(2,1)S(1)}, bf16[256,128]{1,0:T(8,128)(2,1)S(1)}, u32[]{:S(2)}, u32[]{:S(2)}) %collective-permute-start.19) | collective-permute-done | bytes 65568 | tf_op jit(solution)/shard_map/ppermute | solution.py:30
  63.8 0.7 collective-permute-done.20
  64.6 2.9 %collective-permute-start.21 = (bf16[4,256,128]{2,1,0:T(8,128)(2,1)S(1)}, bf16[4,256,128]{2,1,0:T(8,128)(2,1)S(1)}, u32[]{:S(2)}, u32[]{:S(2)}) collective-permute-start(bf16[4,256,128]{2,1,0:T(8,128)(2,1)S(1)} %pad_maximum_fusion.1.p0), channel_id=1, source_target_pairs={{0,16},{8,24},{16,0},{24,8},{32,160},{40,168},{48,176},{56,184},{6... | collective-permute-start | bytes 786440 | tf_op jit(solution)/shard_map/ppermute | solution.py:30
  67.5 2.0 %collective-permute-start.16 = (bf16[256,128]{1,0:T(8,128)(2,1)S(1)}, bf16[256,128]{1,0:T(8,128)(2,1)S(1)}, u32[]{:S(2)}, u32[]{:S(2)}) collective-permute-start(bf16[256,128]{1,0:T(8,128)(2,1)S(1)} %get-tuple-element.56), channel_id=1, source_target_pairs={{0,16},{8,24},{16,0},{24,8},{32,160},{40,168},{48,176},{56,184},{6... | collective-permute-start | bytes 196616 | tf_op jit(solution)/shard_map/ppermute | solution.py:30
  69.5 1.3 %collective-permute-start.17 = (bf16[256,128]{1,0:T(8,128)(2,1)S(1)}, bf16[256,128]{1,0:T(8,128)(2,1)S(1)}, u32[]{:S(2)}, u32[]{:S(2)}) collective-permute-start(bf16[256,128]{1,0:T(8,128)(2,1)S(1)} %get-tuple-element.56), channel_id=1, source_target_pairs={{0,8},{8,16},{16,24},{24,0},{32,96},{40,104},{48,112},{56,120},{64... | collective-permute-start | bytes 196616 | tf_op jit(solution)/shard_map/ppermute | solution.py:30
  70.8 0.8 collective-permute-start.22
  71.6 3.9 %collective-permute-done.15 = bf16[256,128]{1,0:T(8,128)(2,1)S(1)} collective-permute-done((bf16[256,128]{1,0:T(8,128)(2,1)S(1)}, bf16[256,128]{1,0:T(8,128)(2,1)S(1)}, u32[]{:S(2)}, u32[]{:S(2)}) %collective-permute-start.15) | collective-permute-done | bytes 65568 | tf_op jit(solution)/shard_map/ppermute | solution.py:30
  75.5 0.9 collective-permute-start.23
  76.4 0.8 collective-permute-done.16
  77.3 2.3 %collective-permute-start.24 = (bf16[4,256,128]{2,1,0:T(8,128)(2,1)S(1)}, bf16[4,256,128]{2,1,0:T(8,128)(2,1)S(1)}, u32[]{:S(2)}, u32[]{:S(2)}) collective-permute-start(bf16[4,256,128]{2,1,0:T(8,128)(2,1)S(1)} %pad_maximum_fusion.p1), channel_id=1, source_target_pairs={{0,128},{8,136},{16,144},{24,152},{32,48},{40,56},{48,32},{56,40},... | collective-permute-start | bytes 786440 | tf_op jit(solution)/shard_map/ppermute | solution.py:30
  79.6 1.2 %collective-permute-start.25 = (bf16[4,256,128]{2,1,0:T(8,128)(2,1)S(1)}, bf16[4,256,128]{2,1,0:T(8,128)(2,1)S(1)}, u32[]{:S(2)}, u32[]{:S(2)}) collective-permute-start(bf16[4,256,128]{2,1,0:T(8,128)(2,1)S(1)} %pad_maximum_fusion.p1), channel_id=1, source_target_pairs={{0,192},{8,200},{16,208},{24,216},{32,56},{40,32},{48,40},{56,48},... | collective-permute-start | bytes 786440 | tf_op jit(solution)/shard_map/ppermute | solution.py:30
  80.8 0.8 collective-permute-start.26
  81.7 3.6 %shard_map.87 = (bf16[4,512,1024]{2,1,0:T(8,128)(2,1)S(1)}, bf16[4,512,1536]{2,1,0:T(8,128)(2,1)S(1)}, bf16[4,512,1536]{2,1,0:T(8,128)(2,1)S(1)}) custom-call(s32[32]{0:T(128)S(1)} %plan.1.table, s32[4,32]{1,0:T(4,128)S(1)} %copy-done.1, bf16[4,32,256,128]{3,2,1,0:T(8,128)(2,1)S(1)} %bitcast.10, bf16[2,256,128]{2,1,0:T(8,128)(2,1)S(1)} %get-tuple-element.51.after), custom_call_target="tpu_custom_call" | custom-call | flops 2147483648 | bytes 1048576 | tf_op jit(solution)/shard_map/pallas_call | solution.py:254
  85.3 1.9 %shard_map.89 = (f32[4,256,512]{2,1,0:T(8,128)S(1)}, f32[128,2,128]{2,1,0:T(2,128)}) custom-call(bf16[4,512,1024]{2,1,0:T(8,128)(2,1)S(1)} %get-tuple-element.52.weights, f32[256,128]{1,0:T(8,128)S(1)} %get-tuple-element.55.following, bf16[4,256,128]{2,1,0:T(8,128)(2,1)S(1)} %pad_maximum_fusion.p1, bf16[4,256,128]{2,1,0:T(8,128)(2,1)S(1)} %pad_maximum_fusion.1.p0), custom_call_target="tpu_custom_call" | custom-call | flops 1073741824 | bytes 1048576 | tf_op jit(solution)/shard_map/pallas_call | solution.py:275
  87.2 1.8 %shard_map.90.before = f32[4,256,512]{2,1,0:T(8,128)S(1)} custom-call(bf16[4,512,1536]{2,1,0:T(8,128)(2,1)S(1)} %get-tuple-element.60.weights, f32[4,256,512]{2,1,0:T(8,128)S(1)} %get-tuple-element.61.before, bf16[4,256,128]{2,1,0:T(8,128)(2,1)S(1)} %collective-permute-done.21.p1, bf16[4,256,128]{2,1,0:T(8,128)(2,1)S(1)} %collective-permute-done.22.p2, ...), custom_call_target="tpu_custom_call" | custom-call | flops 1610612736 | bytes 1048576 | tf_op jit(solution)/shard_map/pallas_call | solution.py:286
  89.0 2.5 %collective-permute-done.25.p2 = bf16[4,256,128]{2,1,0:T(8,128)(2,1)S(1)} collective-permute-done((bf16[4,256,128]{2,1,0:T(8,128)(2,1)S(1)}, bf16[4,256,128]{2,1,0:T(8,128)(2,1)S(1)}, u32[]{:S(2)}, u32[]{:S(2)}) %collective-permute-start.25) | collective-permute-done | bytes 262176 | tf_op jit(solution)/shard_map/ppermute | solution.py:30
  91.6 1.3 %collective-permute-done.26.p3 = bf16[4,256,128]{2,1,0:T(8,128)(2,1)S(1)} collective-permute-done((bf16[4,256,128]{2,1,0:T(8,128)(2,1)S(1)}, bf16[4,256,128]{2,1,0:T(8,128)(2,1)S(1)}, u32[]{:S(2)}, u32[]{:S(2)}) %collective-permute-start.26) | collective-permute-done | bytes 262176 | tf_op jit(solution)/shard_map/ppermute | solution.py:30
  92.9 3.4 %last.1 = f32[4,256,512]{2,1,0:T(8,128)} custom-call(bf16[4,512,1536]{2,1,0:T(8,128)(2,1)S(1)} %get-tuple-element.59.weights, f32[4,256,512]{2,1,0:T(8,128)S(1)} %shard_map.90.before, bf16[4,256,128]{2,1,0:T(8,128)(2,1)S(1)} %collective-permute-done.24.p1, bf16[4,256,128]{2,1,0:T(8,128)(2,1)S(1)} %collective-permute-done.25.p2, ...), custom_call_target="tpu_custom_call" | custom-call | flops 1610612736 | bytes 1048576 | tf_op jit(solution)/shard_map/last/pallas_call | solution.py:296
  (39 shorter events, 2.8 us)
Async XLA Ops:
  0.6 0.7 copy-start.4
  0.6 1.6 %copy-start.2 = (f32[4,2,128,512]{3,2,1,0:T(8,128)S(1)}, f32[4,2,128,512]{3,2,1,0:T(8,128)}, u32[]{:S(2)}) copy-start(f32[4,2,128,512]{3,2,1,0:T(8,128)} %updates.1) | copy-start | bytes 6291460
  0.6 1.6 %copy-start.3 = (s32[4]{0:T(128)S(1)}, s32[4]{0:T(128)}, u32[]{:S(2)}) copy-start(s32[4]{0:T(128)} %ids.1) | copy-start | bytes 52
  0.7 2.8 %slice-start = ((s8[8388608]{0:T(1024)(128)(4,1)}), s8[4194304]{0:T(1024)(128)(4,1)S(1)}, s32[]{:S(2)}) async-start(s8[8388608]{0:T(1024)(128)(4,1)} %bitcast.9), calls=%async_computation | async-start | bytes 8388608
  2.2 2.7 %slice-start.1 = ((s8[8388608]{0:T(1024)(128)(4,1)}), s8[4194304]{0:T(1024)(128)(4,1)S(1)}, s32[]{:S(2)}) async-start(s8[8388608]{0:T(1024)(128)(4,1)} %bitcast.9), calls=%async_computation.1 | async-start | bytes 8388608
  2.2 2.7 %copy-start.1 = (s32[4,32]{1,0:T(4,128)S(1)}, s32[4,32]{1,0:T(4,128)}, u32[]{:S(2)}) copy-start(s32[4,32]{1,0:T(4,128)} %starts.9) | copy-start | bytes 1540
  10.4 14.3 %collective-permute-start.10 = (bf16[4,256,128]{2,1,0:T(8,128)(2,1)S(1)}, bf16[4,256,128]{2,1,0:T(8,128)(2,1)S(1)}, u32[]{:S(2)}, u32[]{:S(2)}) collective-permute-start(bf16[4,256,128]{2,1,0:T(8,128)(2,1)S(1)} %get-tuple-element.37.after), channel_id=1, source_target_pairs={{0,192},{8,200},{16,208},{24,216},{32,56},{40,32},{48,40},{56,48},... | collective-permute-start | bytes 786440 | tf_op jit(solution)/shard_map/ppermute | solution.py:30
  13.5 15.1 %collective-permute-start.9 = (bf16[4,256,128]{2,1,0:T(8,128)(2,1)S(1)}, bf16[4,256,128]{2,1,0:T(8,128)(2,1)S(1)}, u32[]{:S(2)}, u32[]{:S(2)}) collective-permute-start(bf16[4,256,128]{2,1,0:T(8,128)(2,1)S(1)} %get-tuple-element.36.after), channel_id=1, source_target_pairs={{0,64},{8,72},{16,80},{24,88},{32,40},{40,48},{48,56},{56,32},{64,... | collective-permute-start | bytes 786440 | tf_op jit(solution)/shard_map/ppermute | solution.py:30
  13.5 15.1 %collective-permute-start.8 = (bf16[4,256,128]{2,1,0:T(8,128)(2,1)S(1)}, bf16[4,256,128]{2,1,0:T(8,128)(2,1)S(1)}, u32[]{:S(2)}, u32[]{:S(2)}) collective-permute-start(bf16[4,256,128]{2,1,0:T(8,128)(2,1)S(1)} %get-tuple-element.35.after), channel_id=1, source_target_pairs={{0,128},{8,136},{16,144},{24,152},{32,48},{40,56},{48,32},{56,40},... | collective-permute-start | bytes 786440 | tf_op jit(solution)/shard_map/ppermute | solution.py:30
  15.7 16.7 %collective-permute-start.4 = (bf16[4,256,128]{2,1,0:T(8,128)(2,1)S(1)}, bf16[4,256,128]{2,1,0:T(8,128)(2,1)S(1)}, u32[]{:S(2)}, u32[]{:S(2)}) collective-permute-start(bf16[4,256,128]{2,1,0:T(8,128)(2,1)S(1)} %get-tuple-element.41), channel_id=1, source_target_pairs={{0,24},{8,0},{16,8},{24,16},{32,224},{40,232},{48,240},{56,248},{6... | collective-permute-start | bytes 786440 | tf_op jit(solution)/shard_map/ppermute | solution.py:30
  16.3 17.5 %collective-permute-start.3 = (bf16[4,256,128]{2,1,0:T(8,128)(2,1)S(1)}, bf16[4,256,128]{2,1,0:T(8,128)(2,1)S(1)}, u32[]{:S(2)}, u32[]{:S(2)}) collective-permute-start(bf16[4,256,128]{2,1,0:T(8,128)(2,1)S(1)} %get-tuple-element.40), channel_id=1, source_target_pairs={{0,8},{8,16},{16,24},{24,0},{32,96},{40,104},{48,112},{56,120},{64... | collective-permute-start | bytes 786440 | tf_op jit(solution)/shard_map/ppermute | solution.py:30
  24.7 5.8 %copy-start = (f32[128,2,128]{2,1,0:T(2,128)S(1)}, f32[128,2,128]{2,1,0:T(2,128)}, u32[]{:S(2)}) copy-start(f32[128,2,128]{2,1,0:T(2,128)} %volume.1) | copy-start | bytes 393220
  24.7 10.5 %collective-permute-start.2 = (bf16[4,256,128]{2,1,0:T(8,128)(2,1)S(1)}, bf16[4,256,128]{2,1,0:T(8,128)(2,1)S(1)}, u32[]{:S(2)}, u32[]{:S(2)}) collective-permute-start(bf16[4,256,128]{2,1,0:T(8,128)(2,1)S(1)} %get-tuple-element.39), channel_id=1, source_target_pairs={{0,16},{8,24},{16,0},{24,8},{32,160},{40,168},{48,176},{56,184},{6... | collective-permute-start | bytes 786440 | tf_op jit(solution)/shard_map/ppermute | solution.py:30
  28.8 11.9 %collective-permute-start.11 = (bf16[256,128]{1,0:T(8,128)(2,1)S(1)}, bf16[256,128]{1,0:T(8,128)(2,1)S(1)}, u32[]{:S(2)}, u32[]{:S(2)}) collective-permute-start(bf16[256,128]{1,0:T(8,128)(2,1)S(1)} %get-tuple-element.48), channel_id=1, source_target_pairs={{0,16},{8,24},{16,0},{24,8},{32,160},{40,168},{48,176},{56,184},{6... | collective-permute-start | bytes 196616 | tf_op jit(solution)/shard_map/ppermute | solution.py:30
  31.1 4.8 %collective-permute-start = (f32[2,128]{1,0:T(2,128)S(1)}, f32[2,128]{1,0:T(2,128)S(1)}, u32[]{:S(2)}, u32[]{:S(2)}) collective-permute-start(f32[2,128]{1,0:T(2,128)S(1)} %get-tuple-element.33), channel_id=1, source_target_pairs={{0,1},{1,2},{2,3},{3,4},{4,5},{5,6},{6,7},{8,9},{9,10},{10,11},{11... | collective-permute-start | bytes 3080 | tf_op jit(solution)/shard_map/ppermute | solution.py:315
  32.5 5.2 %collective-permute-start.1 = (f32[2,128]{1,0:T(2,128)S(1)}, f32[2,128]{1,0:T(2,128)S(1)}, u32[]{:S(2)}, u32[]{:S(2)}) collective-permute-start(f32[2,128]{1,0:T(2,128)S(1)} %get-tuple-element.34), channel_id=1, source_target_pairs={{1,0},{2,1},{3,2},{4,3},{5,4},{6,5},{7,6},{9,8},{10,9},{11,10},{12... | collective-permute-start | bytes 3080 | tf_op jit(solution)/shard_map/ppermute | solution.py:316
  33.8 7.5 %collective-permute-start.12 = (bf16[256,128]{1,0:T(8,128)(2,1)S(1)}, bf16[256,128]{1,0:T(8,128)(2,1)S(1)}, u32[]{:S(2)}, u32[]{:S(2)}) collective-permute-start(bf16[256,128]{1,0:T(8,128)(2,1)S(1)} %get-tuple-element.49), channel_id=1, source_target_pairs={{0,8},{8,16},{16,24},{24,0},{32,96},{40,104},{48,112},{56,120},{64... | collective-permute-start | bytes 196616 | tf_op jit(solution)/shard_map/ppermute | solution.py:30
  35.2 6.1 %collective-permute-start.13 = (bf16[256,128]{1,0:T(8,128)(2,1)S(1)}, bf16[256,128]{1,0:T(8,128)(2,1)S(1)}, u32[]{:S(2)}, u32[]{:S(2)}) collective-permute-start(bf16[256,128]{1,0:T(8,128)(2,1)S(1)} %get-tuple-element.50), channel_id=1, source_target_pairs={{0,24},{8,0},{16,8},{24,16},{32,224},{40,232},{48,240},{56,248},{6... | collective-permute-start | bytes 196616 | tf_op jit(solution)/shard_map/ppermute | solution.py:30
  36.0 6.0 %collective-permute-start.5 = (bf16[256,128]{1,0:T(8,128)(2,1)S(1)}, bf16[256,128]{1,0:T(8,128)(2,1)S(1)}, u32[]{:S(2)}, u32[]{:S(2)}) collective-permute-start(bf16[256,128]{1,0:T(8,128)(2,1)S(1)} %get-tuple-element.43), channel_id=1, source_target_pairs={{0,128},{8,136},{16,144},{24,152},{32,48},{40,56},{48,32},{56,40},... | collective-permute-start | bytes 196616 | tf_op jit(solution)/shard_map/ppermute | solution.py:30
  37.7 6.5 %collective-permute-start.6 = (bf16[256,128]{1,0:T(8,128)(2,1)S(1)}, bf16[256,128]{1,0:T(8,128)(2,1)S(1)}, u32[]{:S(2)}, u32[]{:S(2)}) collective-permute-start(bf16[256,128]{1,0:T(8,128)(2,1)S(1)} %get-tuple-element.44), channel_id=1, source_target_pairs={{0,64},{8,72},{16,80},{24,88},{32,40},{40,48},{48,56},{56,32},{64,... | collective-permute-start | bytes 196616 | tf_op jit(solution)/shard_map/ppermute | solution.py:30
  40.7 4.7 %collective-permute-start.7 = (bf16[256,128]{1,0:T(8,128)(2,1)S(1)}, bf16[256,128]{1,0:T(8,128)(2,1)S(1)}, u32[]{:S(2)}, u32[]{:S(2)}) collective-permute-start(bf16[256,128]{1,0:T(8,128)(2,1)S(1)} %get-tuple-element.45), channel_id=1, source_target_pairs={{0,192},{8,200},{16,208},{24,216},{32,56},{40,32},{48,40},{56,48},... | collective-permute-start | bytes 196616 | tf_op jit(solution)/shard_map/ppermute | solution.py:30
  45.4 11.1 %collective-permute-start.14 = (bf16[2,256,128]{2,1,0:T(8,128)(2,1)S(1)}, bf16[2,256,128]{2,1,0:T(8,128)(2,1)S(1)}, u32[]{:S(2)}, u32[]{:S(2)}) collective-permute-start(bf16[2,256,128]{2,1,0:T(8,128)(2,1)S(1)} %get-tuple-element.51.after), channel_id=1, source_target_pairs={{0,32},{8,40},{16,48},{24,56},{32,0},{40,8},{48,16},{56,24},{64,96... | collective-permute-start | bytes 393224 | tf_op jit(solution)/shard_map/ppermute | solution.py:39
  56.5 4.6 %collective-permute-start.18 = (bf16[256,128]{1,0:T(8,128)(2,1)S(1)}, bf16[256,128]{1,0:T(8,128)(2,1)S(1)}, u32[]{:S(2)}, u32[]{:S(2)}) collective-permute-start(bf16[256,128]{1,0:T(8,128)(2,1)S(1)} %get-tuple-element.57), channel_id=1, source_target_pairs={{0,192},{8,200},{16,208},{24,216},{32,56},{40,32},{48,40},{56,48},... | collective-permute-start | bytes 196616 | tf_op jit(solution)/shard_map/ppermute | solution.py:30
  58.0 5.8 %collective-permute-start.19 = (bf16[256,128]{1,0:T(8,128)(2,1)S(1)}, bf16[256,128]{1,0:T(8,128)(2,1)S(1)}, u32[]{:S(2)}, u32[]{:S(2)}) collective-permute-start(bf16[256,128]{1,0:T(8,128)(2,1)S(1)} %get-tuple-element.57), channel_id=1, source_target_pairs={{0,128},{8,136},{16,144},{24,152},{32,48},{40,56},{48,32},{56,40},... | collective-permute-start | bytes 196616 | tf_op jit(solution)/shard_map/ppermute | solution.py:30
  58.7 5.8 %collective-permute-start.20 = (bf16[256,128]{1,0:T(8,128)(2,1)S(1)}, bf16[256,128]{1,0:T(8,128)(2,1)S(1)}, u32[]{:S(2)}, u32[]{:S(2)}) collective-permute-start(bf16[256,128]{1,0:T(8,128)(2,1)S(1)} %get-tuple-element.57), channel_id=1, source_target_pairs={{0,64},{8,72},{16,80},{24,88},{32,40},{40,48},{48,56},{56,32},{64,... | collective-permute-start | bytes 196616 | tf_op jit(solution)/shard_map/ppermute | solution.py:30
  64.6 16.3 %collective-permute-start.21 = (bf16[4,256,128]{2,1,0:T(8,128)(2,1)S(1)}, bf16[4,256,128]{2,1,0:T(8,128)(2,1)S(1)}, u32[]{:S(2)}, u32[]{:S(2)}) collective-permute-start(bf16[4,256,128]{2,1,0:T(8,128)(2,1)S(1)} %pad_maximum_fusion.1.p0), channel_id=1, source_target_pairs={{0,16},{8,24},{16,0},{24,8},{32,160},{40,168},{48,176},{56,184},{6... | collective-permute-start | bytes 786440 | tf_op jit(solution)/shard_map/ppermute | solution.py:30
  67.5 8.0 %collective-permute-start.15 = (bf16[256,128]{1,0:T(8,128)(2,1)S(1)}, bf16[256,128]{1,0:T(8,128)(2,1)S(1)}, u32[]{:S(2)}, u32[]{:S(2)}) collective-permute-start(bf16[256,128]{1,0:T(8,128)(2,1)S(1)} %get-tuple-element.56), channel_id=1, source_target_pairs={{0,24},{8,0},{16,8},{24,16},{32,224},{40,232},{48,240},{56,248},{6... | collective-permute-start | bytes 196616 | tf_op jit(solution)/shard_map/ppermute | solution.py:30
  67.5 9.8 %collective-permute-start.16 = (bf16[256,128]{1,0:T(8,128)(2,1)S(1)}, bf16[256,128]{1,0:T(8,128)(2,1)S(1)}, u32[]{:S(2)}, u32[]{:S(2)}) collective-permute-start(bf16[256,128]{1,0:T(8,128)(2,1)S(1)} %get-tuple-element.56), channel_id=1, source_target_pairs={{0,16},{8,24},{16,0},{24,8},{32,160},{40,168},{48,176},{56,184},{6... | collective-permute-start | bytes 196616 | tf_op jit(solution)/shard_map/ppermute | solution.py:30
  69.5 7.7 %collective-permute-start.17 = (bf16[256,128]{1,0:T(8,128)(2,1)S(1)}, bf16[256,128]{1,0:T(8,128)(2,1)S(1)}, u32[]{:S(2)}, u32[]{:S(2)}) collective-permute-start(bf16[256,128]{1,0:T(8,128)(2,1)S(1)} %get-tuple-element.56), channel_id=1, source_target_pairs={{0,8},{8,16},{16,24},{24,0},{32,96},{40,104},{48,112},{56,120},{64... | collective-permute-start | bytes 196616 | tf_op jit(solution)/shard_map/ppermute | solution.py:30
  70.8 16.4 %collective-permute-start.22 = (bf16[4,256,128]{2,1,0:T(8,128)(2,1)S(1)}, bf16[4,256,128]{2,1,0:T(8,128)(2,1)S(1)}, u32[]{:S(2)}, u32[]{:S(2)}) collective-permute-start(bf16[4,256,128]{2,1,0:T(8,128)(2,1)S(1)} %pad_maximum_fusion.1.p0), channel_id=1, source_target_pairs={{0,24},{8,0},{16,8},{24,16},{32,224},{40,232},{48,240},{56,248},{6... | collective-permute-start | bytes 786440 | tf_op jit(solution)/shard_map/ppermute | solution.py:30
  75.5 11.7 %collective-permute-start.23 = (bf16[4,256,128]{2,1,0:T(8,128)(2,1)S(1)}, bf16[4,256,128]{2,1,0:T(8,128)(2,1)S(1)}, u32[]{:S(2)}, u32[]{:S(2)}) collective-permute-start(bf16[4,256,128]{2,1,0:T(8,128)(2,1)S(1)} %pad_maximum_fusion.1.p0), channel_id=1, source_target_pairs={{0,8},{8,16},{16,24},{24,0},{32,96},{40,104},{48,112},{56,120},{64... | collective-permute-start | bytes 786440 | tf_op jit(solution)/shard_map/ppermute | solution.py:30
  77.3 11.7 %collective-permute-start.24 = (bf16[4,256,128]{2,1,0:T(8,128)(2,1)S(1)}, bf16[4,256,128]{2,1,0:T(8,128)(2,1)S(1)}, u32[]{:S(2)}, u32[]{:S(2)}) collective-permute-start(bf16[4,256,128]{2,1,0:T(8,128)(2,1)S(1)} %pad_maximum_fusion.p1), channel_id=1, source_target_pairs={{0,128},{8,136},{16,144},{24,152},{32,48},{40,56},{48,32},{56,40},... | collective-permute-start | bytes 786440 | tf_op jit(solution)/shard_map/ppermute | solution.py:30
  79.6 11.9 %collective-permute-start.25 = (bf16[4,256,128]{2,1,0:T(8,128)(2,1)S(1)}, bf16[4,256,128]{2,1,0:T(8,128)(2,1)S(1)}, u32[]{:S(2)}, u32[]{:S(2)}) collective-permute-start(bf16[4,256,128]{2,1,0:T(8,128)(2,1)S(1)} %pad_maximum_fusion.p1), channel_id=1, source_target_pairs={{0,192},{8,200},{16,208},{24,216},{32,56},{40,32},{48,40},{56,48},... | collective-permute-start | bytes 786440 | tf_op jit(solution)/shard_map/ppermute | solution.py:30
  80.8 12.1 %collective-permute-start.26 = (bf16[4,256,128]{2,1,0:T(8,128)(2,1)S(1)}, bf16[4,256,128]{2,1,0:T(8,128)(2,1)S(1)}, u32[]{:S(2)}, u32[]{:S(2)}) collective-permute-start(bf16[4,256,128]{2,1,0:T(8,128)(2,1)S(1)} %pad_maximum_fusion.p1), channel_id=1, source_target_pairs={{0,64},{8,72},{16,80},{24,88},{32,40},{40,48},{48,56},{56,32},{64,... | collective-permute-start | bytes 786440 | tf_op jit(solution)/shard_map/ppermute | solution.py:30
